TPU v7x, 128 devices: a whole 4x4x4 slice. The times are simulated.
128 devices in a mesh: group: 4 (over x), seq: 32 (over z, y, core).
Axes of the slice: x: 4, y: 4, z: 4, core: 2. Of those that a mesh axis runs over, the one named last changes fastest.
Arguments:
- tokens: bfloat16 [32, 2048, 2048], P('group', 'seq'), may hold values from -6 to 6
- image_keys: bfloat16 [32, 256, 2048], P('group', 'seq'), may hold values from -256 to 256
- image_values: bfloat16 [32, 256, 2048], P('group', 'seq'), may hold values from -18 to 18
- text_len: int32 [32], replicated, may hold values from 1 to 2048
- image_len: int32 [32], replicated, may hold values from 1 to 256
- counts: int32 [6], replicated, may hold values from 1 to 4, as said below
- old_group: int32 [6], replicated, may hold values from 0 to 3, as said below
- new_group: int32 [6], replicated, may hold values from 0 to 3, as said below
- w_query: bfloat16 [2048, 2048], replicated, may hold values from -0.125 to 0.125
- w_out: bfloat16 [2048, 2048], replicated, may hold values from -0.125 to 0.125
Outputs:
- layer_out: bfloat16 [32, 2048, 2048], P('group', 'seq')
Inputs may be any that keep to these rules, and one draw needn't show every extreme that they name: `counts`: every task has at most 4 samples, and some task has exactly 4. `old_group`: each group is the old group of at most two tasks, and no two tasks share both their old group and their new group, so at most 4 samples go from one old group to one new group. `new_group`: each group is the new group of at most two tasks.
All inputs are finite; a program needn't handle non-finite values.
Results may differ from a plain program's by a relative error of at most 0.011.
Values may be sent and summed in bfloat16 or wider, within the bound.
No kernel may reach another device: no remote copies, remote signals or barrier semaphores. Data moves between devices by JAX's collectives and lax.ppermute only.
A program may use at most 128 MiB of HBM per device.

v0:
```python
import functools

import jax
import jax.numpy as jnp
from jax import lax
from jax.experimental import pallas as pl
from jax.experimental.pallas import tpu as pltpu
from jax.sharding import PartitionSpec as P


HEADS = 16
HEAD_DIM = 128
WIDTH = 2048
GROUPS = 4
SLOTS = 8
TASKS = 6
HALF = 4
RING = 4
CORES = 2
ROWS = 64
KEYS = 8
IMG = 256

masked_score = -1e30
norm_eps = 1e-05


def seq_shift(axis, k):
    pairs = []
    for z in range(RING):
        for y in range(RING):
            for c in range(CORES):
                z2, y2, c2 = z, y, c
                if axis == "z":
                    z2 = (z + k) % RING
                elif axis == "y":
                    y2 = (y + k) % RING
                else:
                    c2 = 1 - c
                pairs.append(((z * RING + y) * CORES + c, (z2 * RING + y2) * CORES + c2))
    return pairs


def move_seq(a, axis, k=1):
    return lax.ppermute(a, "seq", seq_shift(axis, k))


def move_group(a, k):
    return lax.ppermute(a, "group", [(g, (g + k) % GROUPS) for g in range(GROUPS)])


def pack_kernel(
    counts_ref, old_ref, new_ref, text_ref, image_ref, k_ref, v_ref,
    kv0_ref, kv1_ref, kv2_ref, kv3_ref, first_ref, came_ref, head0_ref, head1_ref, index_ref, sem,
):
    group, d = lax.axis_index("group"), lax.axis_index("seq")
    core = d % CORES
    y = (d // CORES) % RING
    z = d // (CORES * RING)
    tasks = range(TASKS)
    count = [counts_ref[t] for t in tasks]
    old = [old_ref[t] for t in tasks]
    new = [new_ref[t] for t in tasks]
    zero = jnp.int32(0)
    start, rank = [], []
    for t in tasks:
        at, before = zero, zero
        for u in range(t):
            at = at + jnp.where(old[u] == old[t], count[u], 0)
            before = before + jnp.where(new[u] == new[t], 1, 0)
        start.append(at)
        rank.append(before)
    copies = []
    for k, out in enumerate((kv0_ref, kv1_ref, kv2_ref, kv3_ref)):
        first = zero
        for t in tasks:
            goes = (old[t] == group) & (new[t] == (group + k) % GROUPS)
            first = jnp.where(goes, start[t], first)
        first_ref[k] = first
        for i, ref in enumerate((k_ref, v_ref)):
            copies.append(
                pltpu.make_async_copy(ref.at[pl.ds(first, HALF)], out.at[i], sem.at[2 * k + i])
            )
            copies[-1].start()
    amounts = []
    for r, head in enumerate((head0_ref, head1_ref)):
        came, amount, base = zero, zero, zero
        for t in tasks:
            mine = (new[t] == group) & (rank[t] == r)
            came = jnp.where(mine, (group - old[t] + GROUPS) % GROUPS, came)
            amount = jnp.where(mine, count[t], amount)
            base = jnp.where(mine, old[t] * SLOTS + start[t], base)
        came_ref[r] = came
        amounts.append(amount)
        head[0], head[1], head[2] = z, y, core
        for j in range(2):
            sample = 2 * core + j
            there = sample < amount
            slot = jnp.where(there, base + sample, 0)
            head[3 + j] = jnp.where(there, image_ref[slot], IMG)
            text = jnp.where(there, text_ref[slot], 0)
            head[5 + 2 * j] = text - d * ROWS
            head[6 + 2 * j] = text - (d + 1 - 2 * core) * ROWS
    for slot in range(SLOTS):
        second = jnp.where(slot >= amounts[0], 1, 0)
        j = slot - second * amounts[0]
        at = jnp.where(j // 2 == core, 0, 4) + 2 * second + j % 2
        index_ref[slot] = jnp.where(slot < amounts[0] + amounts[1], at, -1)
    for copy in copies:
        copy.wait()


def pack(counts, old_group, new_group, text_len, image_len, keys, values):
    smem = pl.BlockSpec(memory_space=pltpu.SMEM)
    vmem = pl.BlockSpec(memory_space=pltpu.VMEM)
    kv = jax.ShapeDtypeStruct((2, HALF, KEYS, WIDTH), jnp.bfloat16)
    ints = [jax.ShapeDtypeStruct((n,), jnp.int32) for n in (4, 2, 9, 9, 8)]
    return pl.pallas_call(
        pack_kernel,
        out_shape=(kv,) * 4 + tuple(ints),
        in_specs=[smem] * 5 + [pl.BlockSpec(memory_space=pltpu.HBM)] * 2,
        out_specs=(vmem,) * 4 + (smem,) * 5,
        scratch_shapes=[pltpu.SemaphoreType.DMA((8,))],
        cost_estimate=pl.CostEstimate(flops=1_000_000, bytes_accessed=2_000_000, transcendentals=0),
    )(counts, old_group, new_group, text_len, image_len, keys, values)


def choose_kernel(came_ref, kv0_ref, kv1_ref, kv2_ref, kv3_ref, mine_ref, send_ref, sem):
    core = lax.axis_index("seq") % CORES
    for r in range(2):
        for k, ref in enumerate((kv0_ref, kv1_ref, kv2_ref, kv3_ref)):

            @pl.when(came_ref[r] == k)
            def _():
                for side, (at, out) in enumerate(((2 * core, mine_ref), (2 - 2 * core, send_ref))):
                    pltpu.make_async_copy(
                        ref.at[:, pl.ds(at, 2)], out.at[r], sem.at[r, side]
                    ).start()

    for r in range(2):
        for side, out in enumerate((mine_ref, send_ref)):
            pltpu.make_async_copy(kv0_ref.at[:, pl.ds(0, 2)], out.at[r], sem.at[r, side]).wait()


def choose(came, parts):
    out = jax.ShapeDtypeStruct((2, 2, 2, KEYS, WIDTH), jnp.bfloat16)
    return pl.pallas_call(
        choose_kernel,
        out_shape=(out, out),
        in_specs=[pl.BlockSpec(memory_space=pltpu.SMEM)] + [pl.BlockSpec(memory_space=pl.ANY)] * 4,
        out_specs=(pl.BlockSpec(memory_space=pltpu.VMEM),) * 2,
        scratch_shapes=[pltpu.SemaphoreType.DMA((2, 2))],
        cost_estimate=pl.CostEstimate(flops=1_000_000, bytes_accessed=1_000_000, transcendentals=0),
    )(came, *parts)


def spread_kernel(first_ref, x_ref, o0_ref, o1_ref, o2_ref, o3_ref, sem):
    copies = [
        pltpu.make_async_copy(x_ref.at[pl.ds(first_ref[k], HALF)], out, sem.at[k])
        for k, out in enumerate((o0_ref, o1_ref, o2_ref, o3_ref))
    ]
    for copy in copies:
        copy.start()
    for copy in copies:
        copy.wait()


def spread(first, tokens):
    out = jax.ShapeDtypeStruct((HALF, ROWS, WIDTH), jnp.bfloat16)
    return pl.pallas_call(
        spread_kernel,
        out_shape=(out,) * 4,
        in_specs=[pl.BlockSpec(memory_space=pltpu.SMEM), pl.BlockSpec(memory_space=pltpu.HBM)],
        out_specs=(pl.BlockSpec(memory_space=pltpu.VMEM),) * 4,
        scratch_shapes=[pltpu.SemaphoreType.DMA((4,))],
        cost_estimate=pl.CostEstimate(flops=1_000_000, bytes_accessed=8_000_000, transcendentals=0),
    )(first, tokens)


def project_kernel(
    came_ref, head_ref, x0_ref, x1_ref, x2_ref, x3_ref, w_ref, mine_ref, send_ref, x, normal, sem,
):
    step = pl.program_id(0)
    core = head_ref[2]

    @pl.when(step == 0)
    def _():
        for r in range(2):
            for k, ref in enumerate((x0_ref, x1_ref, x2_ref, x3_ref)):

                @pl.when(came_ref[r] == k)
                def _():
                    for side, at in ((0, 2 * core), (1, 2 - 2 * core)):
                        pltpu.make_async_copy(
                            ref.at[pl.ds(at, 2)], x.at[pl.ds(4 * side + 2 * r, 2)], sem.at[r, side]
                        ).start()

        for r in range(2):
            for side in range(2):
                pltpu.make_async_copy(
                    x0_ref.at[pl.ds(0, 2)], x.at[pl.ds(4 * side + 2 * r, 2)], sem.at[r, side]
                ).wait()

        def one(i, carry):
            values = x[i].astype(jnp.float32)
            centred = values - jnp.mean(values, axis=-1, keepdims=True)
            variance = jnp.mean(centred * centred, axis=-1, keepdims=True)
            at = pl.multiple_of(i * ROWS, ROWS)
            normal[pl.ds(at, ROWS), :] = (centred * lax.rsqrt(variance + norm_eps)).astype(
                jnp.bfloat16
            )
            return carry

        lax.fori_loop(0, SLOTS, one, 0)

    out = jnp.dot(normal[...], w_ref[...], preferred_element_type=jnp.float32)
    out = (out * HEAD_DIM ** (-0.5)).astype(jnp.bfloat16)
    out = out.reshape(2, 4, ROWS, out.shape[-1])
    mine_ref[...] = out[0]
    send_ref[...] = out[1]


def project(came, head, parts, w_query):
    cols = 512
    smem = pl.BlockSpec(memory_space=pltpu.SMEM)
    out = jax.ShapeDtypeStruct((4, ROWS, WIDTH), jnp.bfloat16)
    o_spec = pl.BlockSpec((4, ROWS, cols), lambda n: (0, 0, n))
    return pl.pallas_call(
        project_kernel,
        out_shape=(out, out),
        grid=(WIDTH // cols,),
        in_specs=[smem, smem]
        + [pl.BlockSpec(memory_space=pl.ANY)] * 4
        + [pl.BlockSpec((WIDTH, cols), lambda n: (0, n))],
        out_specs=(o_spec, o_spec),
        scratch_shapes=[
            pltpu.VMEM((SLOTS, ROWS, WIDTH), jnp.bfloat16),
            pltpu.VMEM((SLOTS * ROWS, WIDTH), jnp.bfloat16),
            pltpu.SemaphoreType.DMA((2, 2)),
        ],
        compiler_params=pltpu.CompilerParams(
            dimension_semantics=("arbitrary",), vmem_limit_bytes=24 * 2**20
        ),
        cost_estimate=pl.CostEstimate(
            flops=4_300_000_000, bytes_accessed=14_000_000, transcendentals=0
        ),
    )(came, head, *parts, w_query)


def attend_kernel(
    rank, head_ref, qm_ref, qt_ref, own_ref, prev_ref, next_ref, opa_ref, opb_ref, w_hbm,
    om_ref, ot_ref, ctx, w, sem,
):
    step = pl.program_id(0)
    copy = pltpu.make_async_copy(w_hbm, w, sem)

    @pl.when(step == 0)
    def _():
        copy.start()

    z, y, core = head_ref[0], head_ref[1], head_ref[2]
    key_limit = jnp.where(step == 0, head_ref[3], head_ref[4])
    i = lax.broadcasted_iota(jnp.int32, (1, IMG), 1)
    run, which, within = i // 64, (i // 16) & 3, i & 15
    hop = jnp.where(run == 1, 3, jnp.where(run == 2, 1, jnp.where(run == 3, 2, 0)))
    back = 4 - which
    at_z = (z + (back if rank == 0 else hop)) & 3
    at_y = (y + (hop if rank == 0 else back)) & 3
    within = (within & 7) + 8 * jnp.where(within < 8, core, 1 - core)
    bias = jnp.where(64 * at_z + 16 * at_y + within < key_limit, 0.0, masked_score)
    row0 = pl.multiple_of(step * (2 * ROWS), 2 * ROWS)
    for h in range(HEADS):
        cols = slice(h * HEAD_DIM, (h + 1) * HEAD_DIM)

        def side(kv):
            return jnp.concatenate(
                [
                    ref[:, kv, :, cols].reshape(-1, HEAD_DIM)
                    for ref in (own_ref, prev_ref, next_ref, opa_ref, opb_ref)
                ],
                axis=0,
            )

        q = jnp.concatenate([qm_ref[0, :, cols], qt_ref[0, :, cols]], axis=0)
        scores = lax.dot_general(
            q, side(0), (((1,), (1,)), ((), ())), preferred_element_type=jnp.float32
        )
        scores = scores + bias
        top = jnp.max(scores, axis=-1, keepdims=True)
        probs = jnp.exp(scores - top)
        total = jnp.sum(probs, axis=-1, keepdims=True)
        mixed = jnp.dot(
            probs.astype(jnp.bfloat16), side(1), preferred_element_type=jnp.float32
        )
        ctx[pl.ds(row0, 2 * ROWS), cols] = (mixed / total).astype(jnp.bfloat16)

    @pl.when(step == 1)
    def _():
        copy.wait()
        row = lax.broadcasted_iota(jnp.int32, (ROWS, 1), 0)
        for n in range(4):
            cols = slice(n * 512, (n + 1) * 512)
            out = jnp.dot(ctx[...], w[:, cols], preferred_element_type=jnp.float32)
            for j in range(2):
                for side, ref in ((0, om_ref), (1, ot_ref)):
                    at = (2 * j + side) * ROWS
                    kept = row < head_ref[5 + 2 * j + side]
                    ref[j, :, cols] = jnp.where(kept, out[at : at + ROWS], 0.0).astype(
                        jnp.bfloat16
                    )


def attend(rank, head, q_mine, q_theirs, pieces, w_out):
    own, prev, after, opa, opb = pieces

    def kv_spec(n):
        return pl.BlockSpec((n, 2, None, 16, WIDTH), lambda j: (0, 0, j, 0, 0))

    q_spec = pl.BlockSpec((1, ROWS, WIDTH), lambda j: (2 * rank + j, 0, 0))
    o_spec = pl.BlockSpec((2, ROWS, WIDTH), lambda j: (0, 0, 0))
    out = jax.ShapeDtypeStruct((2, ROWS, WIDTH), jnp.bfloat16)
    return pl.pallas_call(
        functools.partial(attend_kernel, rank),
        out_shape=(out, out),
        grid=(2,),
        in_specs=[
            pl.BlockSpec(memory_space=pltpu.SMEM),
            q_spec,
            q_spec,
            kv_spec(4),
            kv_spec(4),
            kv_spec(4),
            kv_spec(2),
            kv_spec(2),
            pl.BlockSpec(memory_space=pltpu.HBM),
        ],
        out_specs=(o_spec, o_spec),
        scratch_shapes=[
            pltpu.VMEM((4 * ROWS, WIDTH), jnp.bfloat16),
            pltpu.VMEM((WIDTH, WIDTH), jnp.bfloat16),
            pltpu.SemaphoreType.DMA,
        ],
        compiler_params=pltpu.CompilerParams(
            dimension_semantics=("arbitrary",), vmem_limit_bytes=32 * 2**20
        ),
        cost_estimate=pl.CostEstimate(
            flops=3_500_000_000, bytes_accessed=14_000_000, transcendentals=1_000_000
        ),
    )(head, q_mine, q_theirs, own, prev, after, opa, opb, w_out)


def place_kernel(index_ref, m0_ref, m1_ref, t0_ref, t1_ref, out_ref, zeros, sem):
    zeros[...] = jnp.zeros_like(zeros)
    for slot in range(SLOTS):
        source = index_ref[slot]
        for n, ref in enumerate((m0_ref, m1_ref, t0_ref, t1_ref)):
            for j in range(2):

                @pl.when(source == 2 * n + j)
                def _():
                    pltpu.make_async_copy(ref.at[j], out_ref.at[slot], sem.at[slot]).start()

        @pl.when(source < 0)
        def _():
            pltpu.make_async_copy(zeros, out_ref.at[slot], sem.at[slot]).start()

    for slot in range(SLOTS):
        pltpu.make_async_copy(zeros, out_ref.at[slot], sem.at[slot]).wait()


def place(index, m0, m1, t0, t1):
    return pl.pallas_call(
        place_kernel,
        out_shape=jax.ShapeDtypeStruct((SLOTS, ROWS, WIDTH), jnp.bfloat16),
        in_specs=[pl.BlockSpec(memory_space=pltpu.SMEM)]
        + [pl.BlockSpec(memory_space=pltpu.VMEM)] * 4,
        out_specs=pl.BlockSpec(memory_space=pl.ANY),
        scratch_shapes=[
            pltpu.VMEM((ROWS, WIDTH), jnp.bfloat16),
            pltpu.SemaphoreType.DMA((SLOTS,)),
        ],
        compiler_params=pltpu.CompilerParams(vmem_limit_bytes=8 * 2**20),
        cost_estimate=pl.CostEstimate(
            flops=1_000_000, bytes_accessed=4_000_000, transcendentals=0
        ),
    )(index, m0, m1, t0, t1)


def compute(
    tokens, image_keys, image_values, text_len, image_len, counts, old_group, new_group, w_query, w_out
):
    *kv, first, came, head0, head1, index = pack(
        counts, old_group, new_group, text_len, image_len, image_keys, image_values
    )

    for k in (2, 1, 3):
        kv[k] = move_group(kv[k], k)
    x = list(spread(first, tokens))
    for k in (2, 1, 3):
        x[k] = move_group(x[k], k)

    kv_mine, kv_send = choose(came, kv)
    kv_theirs = move_seq(kv_send, "c")
    block = [jnp.concatenate([kv_mine[r], kv_theirs[r]], axis=2) for r in range(2)]

    quarter = []
    for r, axis in ((0, "z"), (1, "y")):
        parts = [block[r]]
        for k in (1, 2, 3):
            parts.append(move_seq(block[r], axis, k))
        quarter.append(jnp.stack(parts))

    pieces = []
    for r, axis in ((0, "y"), (1, "z")):
        own = quarter[r]
        prev = move_seq(own, axis, 1)
        after = move_seq(own, axis, 3)
        opa = move_seq(prev[:2], axis, 1)
        opb = move_seq(after[2:], axis, 3)
        pieces.append((own, prev, after, opa, opb))

    q_mine, q_send = project(came, head0, x, w_query)
    q_theirs = move_seq(q_send, "c")

    done = []
    for r, head in enumerate((head0, head1)):
        out_mine, out_send = attend(r, head, q_mine, q_theirs, pieces[r], w_out)
        done.append((out_mine, move_seq(out_send, "c")))
    return place(index, done[0][0], done[1][0], done[0][1], done[1][1])


def solution(mesh):
    split = P("group", "seq", None)
    return jax.shard_map(
        compute,
        mesh=mesh,
        in_specs=(split,) * 3 + (P(),) * 7,
        out_specs=split,
        check_vma=False,
    )
```

profile of v0, /device:TPU:1, one launch (start us, length us, event | category | flops | bytes accessed | tf_op | source)
XLA Modules:
  0.0 118.4 jit_solution(3211387249761487726)
XLA Ops:
  0.0 3.3 %shard_map.100 = (bf16[2,4,8,2048]{3,2,1,0:T(8,128)(2,1)}, bf16[2,4,8,2048]{3,2,1,0:T(8,128)(2,1)}, bf16[2,4,8,2048]{3,2,1,0:T(8,128)(2,1)}, bf16[2,4,8,2048]{3,...) custom-call(s32[6]{0:T(128)} %counts_ref.1, s32[6]{0:T(128)} %old_ref.1, ...), custom_call_target="tpu_custom_call" | custom-call | flops 1000000 | bytes 2000000 | tf_op jit(solution)/shard_map/pallas_call | solution.py:118
  3.3 2.1 %collective-permute-start.4 = (bf16[2,4,8,2048]{3,2,1,0:T(8,128)(2,1)}, bf16[2,4,8,2048]{3,2,1,0:T(8,128)(2,1)S(1)}, u32[]{:S(2)}, u32[]{:S(2)}) collective-permute-start(bf16[2,4,8,2048]{3,2,1,0:T(8,128)(2,1)} %get-tuple-element.37), channel_id=1, source_target_pairs={{0,32},{32,64},{64,96},{96,0},{1,33},{33,65},{65,97},{97,1},{2,34}... | collective-permute-start | bytes 786440 | tf_op jit(solution)/shard_map/ppermute | solution.py:49
  5.4 2.4 %collective-permute-start.5 = (bf16[2,4,8,2048]{3,2,1,0:T(8,128)(2,1)}, bf16[2,4,8,2048]{3,2,1,0:T(8,128)(2,1)}, u32[]{:S(2)}, u32[]{:S(2)}) collective-permute-start(bf16[2,4,8,2048]{3,2,1,0:T(8,128)(2,1)} %get-tuple-element.38), channel_id=1, source_target_pairs={{0,64},{32,96},{64,0},{96,32},{1,65},{33,97},{65,1},{97,33},{2,66}... | collective-permute-start | bytes 786440 | tf_op jit(solution)/shard_map/ppermute | solution.py:49
  7.8 1.2 collective-permute-start.6
  8.9 5.3 %shard_map.101 = (bf16[4,64,2048]{2,1,0:T(8,128)(2,1)}, bf16[4,64,2048]{2,1,0:T(8,128)(2,1)}, bf16[4,64,2048]{2,1,0:T(8,128)(2,1)}, bf16[4,64,2048]{2,1,0:T(8,128)(2,1)}) custom-call(s32[4]{0:T(128)} %get-tuple-element.29.first_ref, bf16[8,64,2048]{2,1,0:T(8,128)(2,1)} %x_ref.1), custom_call_target="tpu_custom_call" | custom-call | flops 1000000 | bytes 8000000 | tf_op jit(solution)/shard_map/pallas_call | solution.py:170
  15.3 1.8 %collective-permute-start.2 = (bf16[4,64,2048]{2,1,0:T(8,128)(2,1)}, bf16[4,64,2048]{2,1,0:T(8,128)(2,1)S(1)}, u32[]{:S(2)}, u32[]{:S(2)}) collective-permute-start(bf16[4,64,2048]{2,1,0:T(8,128)(2,1)} %get-tuple-element.33), channel_id=1, source_target_pairs={{0,96},{32,0},{64,32},{96,64},{1,97},{33,1},{65,33},{97,65},{2,98}... | collective-permute-start | bytes 3145736 | tf_op jit(solution)/shard_map/ppermute | solution.py:49
  17.1 2.3 %collective-permute-done.5.kv2_ref = bf16[2,4,8,2048]{3,2,1,0:T(8,128)(2,1)} collective-permute-done((bf16[2,4,8,2048]{3,2,1,0:T(8,128)(2,1)}, bf16[2,4,8,2048]{3,2,1,0:T(8,128)(2,1)}, u32[]{:S(2)}, u32[]{:S(2)}) %collective-permute-start.5) | collective-permute-done | bytes 262176 | tf_op jit(solution)/shard_map/ppermute | solution.py:49
  19.4 2.6 %shard_map.103 = (bf16[2,2,2,8,2048]{4,3,2,1,0:T(8,128)(2,1)}, bf16[2,2,2,8,2048]{4,3,2,1,0:T(8,128)(2,1)}) custom-call(s32[2]{0:T(128)} %get-tuple-element.28.came_ref, bf16[2,4,8,2048]{3,2,1,0:T(8,128)(2,1)} %get-tuple-element.36.kv0_ref, bf16[2,4,8,2048]{3,2,1,0:T(8,128)(2,1)} %copy-done.6, bf16[2,4,8,2048]{3,2,1,0:T(8,128)(2,1)} %collective-permute-done.5.kv2_ref, ...), custom_call_target="tpu_custom_call" | custom-call | flops 1000000 | bytes 1000000 | tf_op jit(solution)/shard_map/pallas_call | solution.py:147
  22.0 2.7 %collective-permute-start.7 = (bf16[2,2,2,8,2048]{4,3,2,1,0:T(8,128)(2,1)}, bf16[2,2,2,8,2048]{4,3,2,1,0:T(8,128)(2,1)S(1)}, u32[]{:S(2)}, u32[]{:S(2)}) collective-permute-start(bf16[2,2,2,8,2048]{4,3,2,1,0:T(8,128)(2,1)} %get-tuple-element.41), channel_id=1, source_target_pairs={{0,1},{1,0},{2,3},{3,2},{4,5},{5,4},{6,7},{7,6},{8,9},{9,8},{10,11... | collective-permute-start | bytes 786440 | tf_op jit(solution)/shard_map/ppermute | solution.py:45
  24.8 1.0 slice_bitcast_fusion.2
  26.2 3.8 %collective-permute-start.10 = (bf16[2,2,16,2048]{3,2,1,0:T(8,128)(2,1)S(1)}, bf16[2,2,16,2048]{3,2,1,0:T(8,128)(2,1)S(1)}, u32[]{:S(2)}, u32[]{:S(2)}) collective-permute-start(bf16[2,2,16,2048]{3,2,1,0:T(8,128)(2,1)S(1)} %get-tuple-element.54), channel_id=1, source_target_pairs={{0,24},{1,25},{2,26},{3,27},{4,28},{5,29},{6,30},{7,31},{8,0},{9,1... | collective-permute-start | bytes 786440 | tf_op jit(solution)/shard_map/ppermute | solution.py:45
  30.1 10.9 %collective-permute-done.10 = bf16[2,2,16,2048]{3,2,1,0:T(8,128)(2,1)S(1)} collective-permute-done((bf16[2,2,16,2048]{3,2,1,0:T(8,128)(2,1)S(1)}, bf16[2,2,16,2048]{3,2,1,0:T(8,128)(2,1)S(1)}, u32[]{:S(2)}, u32[]{:S(2)}) %collective-permute-start.10) | collective-permute-done | bytes 262176 | tf_op jit(solution)/shard_map/ppermute | solution.py:45
  41.0 2.7 %collective-permute-start.17 = (bf16[2,2,16,2048]{3,2,1,0:T(8,128)(2,1)S(1)}, bf16[2,2,16,2048]{3,2,1,0:T(8,128)(2,1)S(1)}, u32[]{:S(2)}, u32[]{:S(2)}) collective-permute-start(bf16[2,2,16,2048]{3,2,1,0:T(8,128)(2,1)S(1)} %get-tuple-element.48), channel_id=1, source_target_pairs={{0,6},{1,7},{2,0},{3,1},{4,2},{5,3},{6,4},{7,5},{8,14},{9,15},{10,... | collective-permute-start | bytes 786440 | tf_op jit(solution)/shard_map/ppermute | solution.py:45
  43.7 6.1 %collective-permute-done.8 = bf16[2,2,16,2048]{3,2,1,0:T(8,128)(2,1)S(1)} collective-permute-done((bf16[2,2,16,2048]{3,2,1,0:T(8,128)(2,1)S(1)}, bf16[2,2,16,2048]{3,2,1,0:T(8,128)(2,1)S(1)}, u32[]{:S(2)}, u32[]{:S(2)}) %collective-permute-start.8) | collective-permute-done | bytes 262176 | tf_op jit(solution)/shard_map/ppermute | solution.py:45
  49.8 2.9 %collective-permute-start.16 = (bf16[2,2,16,2048]{3,2,1,0:T(8,128)(2,1)S(1)}, bf16[2,2,16,2048]{3,2,1,0:T(8,128)(2,1)S(1)}, u32[]{:S(2)}, u32[]{:S(2)}) collective-permute-start(bf16[2,2,16,2048]{3,2,1,0:T(8,128)(2,1)S(1)} %get-tuple-element.48), channel_id=1, source_target_pairs={{0,4},{1,5},{2,6},{3,7},{4,0},{5,1},{6,2},{7,3},{8,12},{9,13},{10,... | collective-permute-start | bytes 786440 | tf_op jit(solution)/shard_map/ppermute | solution.py:45
  53.3 4.1 %collective-permute-done.16 = bf16[2,2,16,2048]{3,2,1,0:T(8,128)(2,1)S(1)} collective-permute-done((bf16[2,2,16,2048]{3,2,1,0:T(8,128)(2,1)S(1)}, bf16[2,2,16,2048]{3,2,1,0:T(8,128)(2,1)S(1)}, u32[]{:S(2)}, u32[]{:S(2)}) %collective-permute-start.16) | collective-permute-done | bytes 262176 | tf_op jit(solution)/shard_map/ppermute | solution.py:45
  57.4 1.3 %collective-permute-start.11 = (bf16[4,2,2,16,2048]{4,3,2,1,0:T(8,128)(2,1)S(1)}, bf16[4,2,2,16,2048]{4,3,2,1,0:T(8,128)(2,1)S(1)}, u32[]{:S(2)}, u32[]{:S(2)}) collective-permute-start(bf16[4,2,2,16,2048]{4,3,2,1,0:T(8,128)(2,1)S(1)} %pad_maximum_fusion.own_ref), channel_id=1, source_target_pairs={{0,2},{1,3},{2,4},{3,5},{4,6},{5,7},{6,0},{7,1},{8,10},{9,11},{10,... | collective-permute-start | bytes 3145736 | tf_op jit(solution)/shard_map/ppermute | solution.py:45
  58.7 5.7 %collective-permute-done.15 = bf16[2,2,16,2048]{3,2,1,0:T(8,128)(2,1)S(1)} collective-permute-done((bf16[2,2,16,2048]{3,2,1,0:T(8,128)(2,1)S(1)}, bf16[2,2,16,2048]{3,2,1,0:T(8,128)(2,1)S(1)}, u32[]{:S(2)}, u32[]{:S(2)}) %collective-permute-start.15) | collective-permute-done | bytes 262176 | tf_op jit(solution)/shard_map/ppermute | solution.py:45
  64.6 3.4 %collective-permute-start.19 = (bf16[4,2,2,16,2048]{4,3,2,1,0:T(8,128)(2,1)S(1)}, bf16[4,2,2,16,2048]{4,3,2,1,0:T(8,128)(2,1)S(1)}, u32[]{:S(2)}, u32[]{:S(2)}) collective-permute-start(bf16[4,2,2,16,2048]{4,3,2,1,0:T(8,128)(2,1)S(1)} %pad_maximum_fusion.1.own_ref), channel_id=1, source_target_pairs={{0,24},{1,25},{2,26},{3,27},{4,28},{5,29},{6,30},{7,31},{8,0},{9,1... | collective-permute-start | bytes 3145736 | tf_op jit(solution)/shard_map/ppermute | solution.py:45
  68.0 3.4 %copy-done.4 = bf16[2048,2048]{1,0:T(8,128)(2,1)S(1)} copy-done((bf16[2048,2048]{1,0:T(8,128)(2,1)S(1)}, bf16[2048,2048]{1,0:T(8,128)(2,1)}, u32[]{:S(2)}) %copy-start.4) | copy-done | bytes 8388632
  71.4 1.2 %copy-done.5 = bf16[4,64,2048]{2,1,0:T(8,128)(2,1)S(1)} copy-done((bf16[4,64,2048]{2,1,0:T(8,128)(2,1)S(1)}, bf16[4,64,2048]{2,1,0:T(8,128)(2,1)}, u32[]{:S(2)}) %copy-start.5) | copy-done | bytes 1048600
  72.7 8.5 %shard_map.102 = (bf16[4,64,2048]{2,1,0:T(8,128)(2,1)S(1)}, bf16[4,64,2048]{2,1,0:T(8,128)(2,1)S(1)}) custom-call(s32[2]{0:T(128)S(1)} %copy-done.3, s32[9]{0:T(128)S(1)} %copy-done.2, bf16[4,64,2048]{2,1,0:T(8,128)(2,1)S(1)} %copy-done.5, bf16[4,64,2048]{2,1,0:T(8,128)(2,1)S(1)} %collective-permute-done.x1_ref, ...), custom_call_target="tpu_custom_call" | custom-call | flops 4300000256 | bytes 14000000 | tf_op jit(solution)/shard_map/pallas_call | solution.py:228
  81.2 4.0 %collective-permute-start.3 = (bf16[4,64,2048]{2,1,0:T(8,128)(2,1)S(1)}, bf16[4,64,2048]{2,1,0:T(8,128)(2,1)S(1)}, u32[]{:S(2)}, u32[]{:S(2)}) collective-permute-start(bf16[4,64,2048]{2,1,0:T(8,128)(2,1)S(1)} %get-tuple-element.35), channel_id=1, source_target_pairs={{0,1},{1,0},{2,3},{3,2},{4,5},{5,4},{6,7},{7,6},{8,9},{9,8},{10,11... | collective-permute-start | bytes 3145736 | tf_op jit(solution)/shard_map/ppermute | solution.py:45
  85.2 1.1 collective-permute-done.11.prev_ref
  87.2 2.1 %collective-permute-start.14 = (bf16[2,2,2,16,2048]{4,3,2,1,0:T(8,128)(2,1)S(1)}, bf16[2,2,2,16,2048]{4,3,2,1,0:T(8,128)(2,1)S(1)}, u32[]{:S(2)}, u32[]{:S(2)}) collective-permute-start(bf16[2,2,2,16,2048]{4,3,2,1,0:T(8,128)(2,1)S(1)} %slice.34), channel_id=1, source_target_pairs={{0,6},{1,7},{2,0},{3,1},{4,2},{5,3},{6,4},{7,5},{8,14},{9,15},{10,... | collective-permute-start | bytes 1572872 | tf_op jit(solution)/shard_map/ppermute | solution.py:45
  89.8 2.5 %collective-permute-start.21 = (bf16[2,2,2,16,2048]{4,3,2,1,0:T(8,128)(2,1)S(1)}, bf16[2,2,2,16,2048]{4,3,2,1,0:T(8,128)(2,1)S(1)}, u32[]{:S(2)}, u32[]{:S(2)}) collective-permute-start(bf16[2,2,2,16,2048]{4,3,2,1,0:T(8,128)(2,1)S(1)} %slice.37), channel_id=1, source_target_pairs={{0,24},{1,25},{2,26},{3,27},{4,28},{5,29},{6,30},{7,31},{8,0},{9,1... | collective-permute-start | bytes 1572872 | tf_op jit(solution)/shard_map/ppermute | solution.py:45
  92.4 7.0 %collective-permute-done.13.opa_ref = bf16[2,2,2,16,2048]{4,3,2,1,0:T(8,128)(2,1)S(1)} collective-permute-done((bf16[2,2,2,16,2048]{4,3,2,1,0:T(8,128)(2,1)S(1)}, bf16[2,2,2,16,2048]{4,3,2,1,0:T(8,128)(2,1)S(1)}, u32[]{:S(2)}, u32[]{:S(2)}) %collective-permute-start.13) | collective-permute-done | bytes 524320 | tf_op jit(solution)/shard_map/ppermute | solution.py:45
  99.3 6.1 %shard_map.104 = (bf16[2,64,2048]{2,1,0:T(8,128)(2,1)S(1)}, bf16[2,64,2048]{2,1,0:T(8,128)(2,1)S(1)}) custom-call(s32[9]{0:T(128)S(1)} %copy-done.2, bf16[4,64,2048]{2,1,0:T(8,128)(2,1)S(1)} %get-tuple-element.34.qm_ref, bf16[4,64,2048]{2,1,0:T(8,128)(2,1)S(1)} %collective-permute-done.3.qt_ref, bf16[4,2,2,16,2048]{4,3,2,1,0:T(8,128)(2,1)S(1)} %pad_maximum_fusion.own_ref, ...), custom_call_target="tpu_custom_call" | custom-call | flops 3500000000 | bytes 14000000 | tf_op jit(solution)/shard_map/pallas_call | solution.py:322
  105.4 2.7 %collective-permute-start.22 = (bf16[2,64,2048]{2,1,0:T(8,128)(2,1)S(1)}, bf16[2,64,2048]{2,1,0:T(8,128)(2,1)S(1)}, u32[]{:S(2)}, u32[]{:S(2)}) collective-permute-start(bf16[2,64,2048]{2,1,0:T(8,128)(2,1)S(1)} %get-tuple-element.45), channel_id=1, source_target_pairs={{0,1},{1,0},{2,3},{3,2},{4,5},{5,4},{6,7},{7,6},{8,9},{9,8},{10,11... | collective-permute-start | bytes 1572872 | tf_op jit(solution)/shard_map/ppermute | solution.py:45
  108.2 6.1 %shard_map.105 = (bf16[2,64,2048]{2,1,0:T(8,128)(2,1)S(1)}, bf16[2,64,2048]{2,1,0:T(8,128)(2,1)S(1)}) custom-call(s32[9]{0:T(128)S(1)} %copy-done.1, bf16[4,64,2048]{2,1,0:T(8,128)(2,1)S(1)} %get-tuple-element.34.qm_ref, bf16[4,64,2048]{2,1,0:T(8,128)(2,1)S(1)} %collective-permute-done.3.qt_ref, bf16[4,2,2,16,2048]{4,3,2,1,0:T(8,128)(2,1)S(1)} %pad_maximum_fusion.1.own_ref, ...), custom_call_target="tpu_custom_call" | custom-call | flops 3500000000 | bytes 14000000 | tf_op jit(solution)/shard_map/pallas_call | solution.py:322
  114.4 1.9 %collective-permute-done.23.t1_ref = bf16[2,64,2048]{2,1,0:T(8,128)(2,1)S(1)} collective-permute-done((bf16[2,64,2048]{2,1,0:T(8,128)(2,1)S(1)}, bf16[2,64,2048]{2,1,0:T(8,128)(2,1)S(1)}, u32[]{:S(2)}, u32[]{:S(2)}) %collective-permute-start.23) | collective-permute-done | bytes 524320 | tf_op jit(solution)/shard_map/ppermute | solution.py:45
  116.3 1.9 %shard_map.106 = bf16[8,64,2048]{2,1,0:T(8,128)(2,1)} custom-call(s32[8]{0:T(128)S(1)} %copy-done, bf16[2,64,2048]{2,1,0:T(8,128)(2,1)S(1)} %get-tuple-element.42.m0_ref, bf16[2,64,2048]{2,1,0:T(8,128)(2,1)S(1)} %get-tuple-element.44.m1_ref, bf16[2,64,2048]{2,1,0:T(8,128)(2,1)S(1)} %collective-permute-done.22.t0_ref, ...), custom_call_target="tpu_custom_call" | custom-call | flops 1000000 | bytes 4000000 | tf_op jit(solution)/shard_map/pallas_call | solution.py:372
  (52 shorter events, 3.8 us)
Async XLA Ops:
  3.3 64.8 %copy-start.2 = (s32[9]{0:T(128)S(1)}, s32[9]{0:T(128)}, u32[]{:S(2)}) copy-start(s32[9]{0:T(128)} %get-tuple-element.27.head_ref) | copy-start | bytes 112
  3.3 64.8 %copy-start.3 = (s32[2]{0:T(128)S(1)}, s32[2]{0:T(128)}, u32[]{:S(2)}) copy-start(s32[2]{0:T(128)} %get-tuple-element.28.came_ref) | copy-start | bytes 28
  3.3 12.0 %collective-permute-start.4 = (bf16[2,4,8,2048]{3,2,1,0:T(8,128)(2,1)}, bf16[2,4,8,2048]{3,2,1,0:T(8,128)(2,1)S(1)}, u32[]{:S(2)}, u32[]{:S(2)}) collective-permute-start(bf16[2,4,8,2048]{3,2,1,0:T(8,128)(2,1)} %get-tuple-element.37), channel_id=1, source_target_pairs={{0,32},{32,64},{64,96},{96,0},{1,33},{33,65},{65,97},{97,1},{2,34}... | collective-permute-start | bytes 786440 | tf_op jit(solution)/shard_map/ppermute | solution.py:49
  5.4 14.0 %collective-permute-start.5 = (bf16[2,4,8,2048]{3,2,1,0:T(8,128)(2,1)}, bf16[2,4,8,2048]{3,2,1,0:T(8,128)(2,1)}, u32[]{:S(2)}, u32[]{:S(2)}) collective-permute-start(bf16[2,4,8,2048]{3,2,1,0:T(8,128)(2,1)} %get-tuple-element.38), channel_id=1, source_target_pairs={{0,64},{32,96},{64,0},{96,32},{1,65},{33,97},{65,1},{97,33},{2,66}... | collective-permute-start | bytes 786440 | tf_op jit(solution)/shard_map/ppermute | solution.py:49
  7.8 11.7 %collective-permute-start.6 = (bf16[2,4,8,2048]{3,2,1,0:T(8,128)(2,1)}, bf16[2,4,8,2048]{3,2,1,0:T(8,128)(2,1)}, u32[]{:S(2)}, u32[]{:S(2)}) collective-permute-start(bf16[2,4,8,2048]{3,2,1,0:T(8,128)(2,1)} %get-tuple-element.39), channel_id=1, source_target_pairs={{0,96},{32,0},{64,32},{96,64},{1,97},{33,1},{65,33},{97,65},{2,98}... | collective-permute-start | bytes 786440 | tf_op jit(solution)/shard_map/ppermute | solution.py:49
  14.2 50.3 %collective-permute-start = (bf16[4,64,2048]{2,1,0:T(8,128)(2,1)}, bf16[4,64,2048]{2,1,0:T(8,128)(2,1)S(1)}, u32[]{:S(2)}, u32[]{:S(2)}) collective-permute-start(bf16[4,64,2048]{2,1,0:T(8,128)(2,1)} %get-tuple-element.31), channel_id=1, source_target_pairs={{0,32},{32,64},{64,96},{96,0},{1,33},{33,65},{65,97},{97,1},{2,34}... | collective-permute-start | bytes 3145736 | tf_op jit(solution)/shard_map/ppermute | solution.py:49
  14.6 50.0 %collective-permute-start.1 = (bf16[4,64,2048]{2,1,0:T(8,128)(2,1)}, bf16[4,64,2048]{2,1,0:T(8,128)(2,1)S(1)}, u32[]{:S(2)}, u32[]{:S(2)}) collective-permute-start(bf16[4,64,2048]{2,1,0:T(8,128)(2,1)} %get-tuple-element.32), channel_id=1, source_target_pairs={{0,64},{32,96},{64,0},{96,32},{1,65},{33,97},{65,1},{97,33},{2,66}... | collective-permute-start | bytes 3145736 | tf_op jit(solution)/shard_map/ppermute | solution.py:49
  15.3 4.2 %copy-start.6 = (bf16[2,4,8,2048]{3,2,1,0:T(8,128)(2,1)}, bf16[2,4,8,2048]{3,2,1,0:T(8,128)(2,1)S(1)}, u32[]{:S(2)}) copy-start(bf16[2,4,8,2048]{3,2,1,0:T(8,128)(2,1)S(1)} %collective-permute-done.4.kv1_ref) | copy-start | bytes 786436
  15.3 52.8 %collective-permute-start.2 = (bf16[4,64,2048]{2,1,0:T(8,128)(2,1)}, bf16[4,64,2048]{2,1,0:T(8,128)(2,1)S(1)}, u32[]{:S(2)}, u32[]{:S(2)}) collective-permute-start(bf16[4,64,2048]{2,1,0:T(8,128)(2,1)} %get-tuple-element.33), channel_id=1, source_target_pairs={{0,96},{32,0},{64,32},{96,64},{1,97},{33,1},{65,33},{97,65},{2,98}... | collective-permute-start | bytes 3145736 | tf_op jit(solution)/shard_map/ppermute | solution.py:49
  22.0 4.1 %collective-permute-start.7 = (bf16[2,2,2,8,2048]{4,3,2,1,0:T(8,128)(2,1)}, bf16[2,2,2,8,2048]{4,3,2,1,0:T(8,128)(2,1)S(1)}, u32[]{:S(2)}, u32[]{:S(2)}) collective-permute-start(bf16[2,2,2,8,2048]{4,3,2,1,0:T(8,128)(2,1)} %get-tuple-element.41), channel_id=1, source_target_pairs={{0,1},{1,0},{2,3},{3,2},{4,5},{5,4},{6,7},{7,6},{8,9},{9,8},{10,11... | collective-permute-start | bytes 786440 | tf_op jit(solution)/shard_map/ppermute | solution.py:45
  26.2 14.7 %collective-permute-start.10 = (bf16[2,2,16,2048]{3,2,1,0:T(8,128)(2,1)S(1)}, bf16[2,2,16,2048]{3,2,1,0:T(8,128)(2,1)S(1)}, u32[]{:S(2)}, u32[]{:S(2)}) collective-permute-start(bf16[2,2,16,2048]{3,2,1,0:T(8,128)(2,1)S(1)} %get-tuple-element.54), channel_id=1, source_target_pairs={{0,24},{1,25},{2,26},{3,27},{4,28},{5,29},{6,30},{7,31},{8,0},{9,1... | collective-permute-start | bytes 786440 | tf_op jit(solution)/shard_map/ppermute | solution.py:45
  30.1 10.9 %collective-permute-start.9 = (bf16[2,2,16,2048]{3,2,1,0:T(8,128)(2,1)S(1)}, bf16[2,2,16,2048]{3,2,1,0:T(8,128)(2,1)S(1)}, u32[]{:S(2)}, u32[]{:S(2)}) collective-permute-start(bf16[2,2,16,2048]{3,2,1,0:T(8,128)(2,1)S(1)} %get-tuple-element.54), channel_id=1, source_target_pairs={{0,16},{1,17},{2,18},{3,19},{4,20},{5,21},{6,22},{7,23},{8,24},{9,... | collective-permute-start | bytes 786440 | tf_op jit(solution)/shard_map/ppermute | solution.py:45
  41.0 8.9 %collective-permute-start.8 = (bf16[2,2,16,2048]{3,2,1,0:T(8,128)(2,1)S(1)}, bf16[2,2,16,2048]{3,2,1,0:T(8,128)(2,1)S(1)}, u32[]{:S(2)}, u32[]{:S(2)}) collective-permute-start(bf16[2,2,16,2048]{3,2,1,0:T(8,128)(2,1)S(1)} %get-tuple-element.54), channel_id=1, source_target_pairs={{0,8},{1,9},{2,10},{3,11},{4,12},{5,13},{6,14},{7,15},{8,16},{9,17... | collective-permute-start | bytes 786440 | tf_op jit(solution)/shard_map/ppermute | solution.py:45
  41.0 11.8 %collective-permute-start.17 = (bf16[2,2,16,2048]{3,2,1,0:T(8,128)(2,1)S(1)}, bf16[2,2,16,2048]{3,2,1,0:T(8,128)(2,1)S(1)}, u32[]{:S(2)}, u32[]{:S(2)}) collective-permute-start(bf16[2,2,16,2048]{3,2,1,0:T(8,128)(2,1)S(1)} %get-tuple-element.48), channel_id=1, source_target_pairs={{0,6},{1,7},{2,0},{3,1},{4,2},{5,3},{6,4},{7,5},{8,14},{9,15},{10,... | collective-permute-start | bytes 786440 | tf_op jit(solution)/shard_map/ppermute | solution.py:45
  49.8 7.6 %collective-permute-start.16 = (bf16[2,2,16,2048]{3,2,1,0:T(8,128)(2,1)S(1)}, bf16[2,2,16,2048]{3,2,1,0:T(8,128)(2,1)S(1)}, u32[]{:S(2)}, u32[]{:S(2)}) collective-permute-start(bf16[2,2,16,2048]{3,2,1,0:T(8,128)(2,1)S(1)} %get-tuple-element.48), channel_id=1, source_target_pairs={{0,4},{1,5},{2,6},{3,7},{4,0},{5,1},{6,2},{7,3},{8,12},{9,13},{10,... | collective-permute-start | bytes 786440 | tf_op jit(solution)/shard_map/ppermute | solution.py:45
  52.7 11.6 %collective-permute-start.15 = (bf16[2,2,16,2048]{3,2,1,0:T(8,128)(2,1)S(1)}, bf16[2,2,16,2048]{3,2,1,0:T(8,128)(2,1)S(1)}, u32[]{:S(2)}, u32[]{:S(2)}) collective-permute-start(bf16[2,2,16,2048]{3,2,1,0:T(8,128)(2,1)S(1)} %get-tuple-element.48), channel_id=1, source_target_pairs={{0,2},{1,3},{2,4},{3,5},{4,6},{5,7},{6,0},{7,1},{8,10},{9,11},{10,... | collective-permute-start | bytes 786440 | tf_op jit(solution)/shard_map/ppermute | solution.py:45
  57.4 28.9 %collective-permute-start.11 = (bf16[4,2,2,16,2048]{4,3,2,1,0:T(8,128)(2,1)S(1)}, bf16[4,2,2,16,2048]{4,3,2,1,0:T(8,128)(2,1)S(1)}, u32[]{:S(2)}, u32[]{:S(2)}) collective-permute-start(bf16[4,2,2,16,2048]{4,3,2,1,0:T(8,128)(2,1)S(1)} %pad_maximum_fusion.own_ref), channel_id=1, source_target_pairs={{0,2},{1,3},{2,4},{3,5},{4,6},{5,7},{6,0},{7,1},{8,10},{9,11},{10,... | collective-permute-start | bytes 3145736 | tf_op jit(solution)/shard_map/ppermute | solution.py:45
  64.4 22.7 %collective-permute-start.12 = (bf16[4,2,2,16,2048]{4,3,2,1,0:T(8,128)(2,1)S(1)}, bf16[4,2,2,16,2048]{4,3,2,1,0:T(8,128)(2,1)S(1)}, u32[]{:S(2)}, u32[]{:S(2)}) collective-permute-start(bf16[4,2,2,16,2048]{4,3,2,1,0:T(8,128)(2,1)S(1)} %pad_maximum_fusion.own_ref), channel_id=1, source_target_pairs={{0,6},{1,7},{2,0},{3,1},{4,2},{5,3},{6,4},{7,5},{8,14},{9,15},{10,... | collective-permute-start | bytes 3145736 | tf_op jit(solution)/shard_map/ppermute | solution.py:45
  64.4 35.0 %slice-start = ((s8[8388608]{0:T(1024)(128)(4,1)}), s8[4194304]{0:T(1024)(128)(4,1)S(1)}, s32[]{:S(2)}) async-start(s8[8388608]{0:T(1024)(128)(4,1)} %bitcast.18), calls=%async_computation | async-start | bytes 8388608
  64.5 24.7 %collective-permute-start.18 = (bf16[4,2,2,16,2048]{4,3,2,1,0:T(8,128)(2,1)S(1)}, bf16[4,2,2,16,2048]{4,3,2,1,0:T(8,128)(2,1)S(1)}, u32[]{:S(2)}, u32[]{:S(2)}) collective-permute-start(bf16[4,2,2,16,2048]{4,3,2,1,0:T(8,128)(2,1)S(1)} %pad_maximum_fusion.1.own_ref), channel_id=1, source_target_pairs={{0,8},{1,9},{2,10},{3,11},{4,12},{5,13},{6,14},{7,15},{8,16},{9,17... | collective-permute-start | bytes 3145736 | tf_op jit(solution)/shard_map/ppermute | solution.py:45
  64.6 25.2 %collective-permute-start.19 = (bf16[4,2,2,16,2048]{4,3,2,1,0:T(8,128)(2,1)S(1)}, bf16[4,2,2,16,2048]{4,3,2,1,0:T(8,128)(2,1)S(1)}, u32[]{:S(2)}, u32[]{:S(2)}) collective-permute-start(bf16[4,2,2,16,2048]{4,3,2,1,0:T(8,128)(2,1)S(1)} %pad_maximum_fusion.1.own_ref), channel_id=1, source_target_pairs={{0,24},{1,25},{2,26},{3,27},{4,28},{5,29},{6,30},{7,31},{8,0},{9,1... | collective-permute-start | bytes 3145736 | tf_op jit(solution)/shard_map/ppermute | solution.py:45
  68.0 3.4 %copy-start.4 = (bf16[2048,2048]{1,0:T(8,128)(2,1)S(1)}, bf16[2048,2048]{1,0:T(8,128)(2,1)}, u32[]{:S(2)}) copy-start(bf16[2048,2048]{1,0:T(8,128)(2,1)} %w_ref.1) | copy-start | bytes 25165828
  72.6 26.7 %slice-start.1 = ((s8[8388608]{0:T(1024)(128)(4,1)}), s8[4194304]{0:T(1024)(128)(4,1)S(1)}, s32[]{:S(2)}) async-start(s8[8388608]{0:T(1024)(128)(4,1)} %bitcast.18), calls=%async_computation.1 | async-start | bytes 8388608
  81.2 11.2 %collective-permute-start.3 = (bf16[4,64,2048]{2,1,0:T(8,128)(2,1)S(1)}, bf16[4,64,2048]{2,1,0:T(8,128)(2,1)S(1)}, u32[]{:S(2)}, u32[]{:S(2)}) collective-permute-start(bf16[4,64,2048]{2,1,0:T(8,128)(2,1)S(1)} %get-tuple-element.35), channel_id=1, source_target_pairs={{0,1},{1,0},{2,3},{3,2},{4,5},{5,4},{6,7},{7,6},{8,9},{9,8},{10,11... | collective-permute-start | bytes 3145736 | tf_op jit(solution)/shard_map/ppermute | solution.py:45
  86.4 12.9 %collective-permute-start.13 = (bf16[2,2,2,16,2048]{4,3,2,1,0:T(8,128)(2,1)S(1)}, bf16[2,2,2,16,2048]{4,3,2,1,0:T(8,128)(2,1)S(1)}, u32[]{:S(2)}, u32[]{:S(2)}) collective-permute-start(bf16[2,2,2,16,2048]{4,3,2,1,0:T(8,128)(2,1)S(1)} %slice.33), channel_id=1, source_target_pairs={{0,2},{1,3},{2,4},{3,5},{4,6},{5,7},{6,0},{7,1},{8,10},{9,11},{10,... | collective-permute-start | bytes 1572872 | tf_op jit(solution)/shard_map/ppermute | solution.py:45
  87.1 21.1 %copy-start.1 = (s32[9]{0:T(128)S(1)}, s32[9]{0:T(128)}, u32[]{:S(2)}) copy-start(s32[9]{0:T(128)} %get-tuple-element.43.head_ref) | copy-start | bytes 112
  87.2 12.2 %collective-permute-start.14 = (bf16[2,2,2,16,2048]{4,3,2,1,0:T(8,128)(2,1)S(1)}, bf16[2,2,2,16,2048]{4,3,2,1,0:T(8,128)(2,1)S(1)}, u32[]{:S(2)}, u32[]{:S(2)}) collective-permute-start(bf16[2,2,2,16,2048]{4,3,2,1,0:T(8,128)(2,1)S(1)} %slice.34), channel_id=1, source_target_pairs={{0,6},{1,7},{2,0},{3,1},{4,2},{5,3},{6,4},{7,5},{8,14},{9,15},{10,... | collective-permute-start | bytes 1572872 | tf_op jit(solution)/shard_map/ppermute | solution.py:45
  89.3 18.9 %collective-permute-start.20 = (bf16[2,2,2,16,2048]{4,3,2,1,0:T(8,128)(2,1)S(1)}, bf16[2,2,2,16,2048]{4,3,2,1,0:T(8,128)(2,1)S(1)}, u32[]{:S(2)}, u32[]{:S(2)}) collective-permute-start(bf16[2,2,2,16,2048]{4,3,2,1,0:T(8,128)(2,1)S(1)} %slice.36), channel_id=1, source_target_pairs={{0,8},{1,9},{2,10},{3,11},{4,12},{5,13},{6,14},{7,15},{8,16},{9,17... | collective-permute-start | bytes 1572872 | tf_op jit(solution)/shard_map/ppermute | solution.py:45
  89.8 18.4 %collective-permute-start.21 = (bf16[2,2,2,16,2048]{4,3,2,1,0:T(8,128)(2,1)S(1)}, bf16[2,2,2,16,2048]{4,3,2,1,0:T(8,128)(2,1)S(1)}, u32[]{:S(2)}, u32[]{:S(2)}) collective-permute-start(bf16[2,2,2,16,2048]{4,3,2,1,0:T(8,128)(2,1)S(1)} %slice.37), channel_id=1, source_target_pairs={{0,24},{1,25},{2,26},{3,27},{4,28},{5,29},{6,30},{7,31},{8,0},{9,1... | collective-permute-start | bytes 1572872 | tf_op jit(solution)/shard_map/ppermute | solution.py:45
  105.4 10.9 %copy-start = (s32[8]{0:T(128)S(1)}, s32[8]{0:T(128)}, u32[]{:S(2)}) copy-start(s32[8]{0:T(128)} %get-tuple-element.26.index_ref) | copy-start | bytes 100
  105.4 9.0 %collective-permute-start.22 = (bf16[2,64,2048]{2,1,0:T(8,128)(2,1)S(1)}, bf16[2,64,2048]{2,1,0:T(8,128)(2,1)S(1)}, u32[]{:S(2)}, u32[]{:S(2)}) collective-permute-start(bf16[2,64,2048]{2,1,0:T(8,128)(2,1)S(1)} %get-tuple-element.45), channel_id=1, source_target_pairs={{0,1},{1,0},{2,3},{3,2},{4,5},{5,4},{6,7},{7,6},{8,9},{9,8},{10,11... | collective-permute-start | bytes 1572872 | tf_op jit(solution)/shard_map/ppermute | solution.py:45
  114.3 2.0 %collective-permute-start.23 = (bf16[2,64,2048]{2,1,0:T(8,128)(2,1)S(1)}, bf16[2,64,2048]{2,1,0:T(8,128)(2,1)S(1)}, u32[]{:S(2)}, u32[]{:S(2)}) collective-permute-start(bf16[2,64,2048]{2,1,0:T(8,128)(2,1)S(1)} %get-tuple-element.46), channel_id=1, source_target_pairs={{0,1},{1,0},{2,3},{3,2},{4,5},{5,4},{6,7},{7,6},{8,9},{9,8},{10,11... | collective-permute-start | bytes 1572872 | tf_op jit(solution)/shard_map/ppermute | solution.py:45
  (1 other events, 1.2 us)
where the time goes:
time: 119 us; the launch traced here: 118 us
  waiting for transfers between devices  39.5 us (33%)
  starting transfers between devices  38.6 us (32%)
  Pallas kernels  33.7 us (28%)
  local copies, waits for them, and re-layouts  5.79 us (5%)
    ppermute x18, waiting for transfers between devices, move_seq(): return lax.ppermute(a, 'seq', seq_shift(axis, k))  37.2 us
    ppermute x18, starting transfers between devices, move_seq(): return lax.ppermute(a, 'seq', seq_shift(axis, k))  30.1 us
    pallas_call x2, Pallas kernels, attend(): pl.pallas_call(functools.partial(attend_kernel, rank), out_shape=(out, ou...  12.2 us
    pallas_call x1, Pallas kernels, project(): pl.pallas_call(project_kernel, out_shape=(out, out), grid=(WIDTH // cols,...  8.51 us
    ppermute x6, starting transfers between devices, move_group(): lax.ppermute(a, 'group', [(g, (g + k) % GROUPS) for g in range(GROUPS)])  8.51 us
    pallas_call x1, Pallas kernels, spread(): pl.pallas_call(spread_kernel, out_shape=(out,) * 4, in_specs=[pl.BlockSpe...  5.3 us
    unnamed x18, local copies, waits for them, and re-layouts  4.63 us
    pallas_call x1, Pallas kernels, pack(): pl.pallas_call(pack_kernel, out_shape=(kv,) * 4 + tuple(ints), in_specs=[...  3.26 us
  transfers between devices with their start and end apart: 24, of which 9 were waited for; matrix products, arithmetic and copies ran while one was open for 1% of the time, Pallas kernels for 24%

commit v1 on v0

v1 whole, which is shorter than its diff:
```python
import functools

import jax
import jax.numpy as jnp
from jax import lax
from jax.experimental import pallas as pl
from jax.experimental.pallas import tpu as pltpu
from jax.sharding import PartitionSpec as P


HEADS = 16
HEAD_DIM = 128
WIDTH = 2048
GROUPS = 4
SLOTS = 8
TASKS = 6
HALF = 4
RING = 4
CORES = 2
ROWS = 64
PART = 32
KEYS = 8
IMG = 256

masked_score = -1e30
norm_eps = 1e-05


def seq_moves(phase, k):
    pairs = []
    for z in range(RING):
        for y in range(RING):
            for c in range(CORES):
                z2, y2, c2 = z, y, c
                if phase == "swap":
                    c2 = 1 - c
                elif (phase == "near") == (c == 0):
                    z2 = (z + k) % RING
                else:
                    y2 = (y + k) % RING
                pairs.append(((z * RING + y) * CORES + c, (z2 * RING + y2) * CORES + c2))
    return pairs


def move_seq(a, phase, k=1):
    return lax.ppermute(a, "seq", seq_moves(phase, k))


def move_group(a, k):
    return lax.ppermute(a, "group", [(g, (g + k) % GROUPS) for g in range(GROUPS)])


def pack_kernel(
    counts_ref, old_ref, new_ref, text_ref, image_ref, k_ref, v_ref,
    kv0_ref, kv1_ref, kv2_ref, kv3_ref, first_ref, came_ref, head0_ref, head1_ref, index_ref, sem,
):
    group, d = lax.axis_index("group"), lax.axis_index("seq")
    core = d % CORES
    y = (d // CORES) % RING
    z = d // (CORES * RING)
    tasks = range(TASKS)
    count = [counts_ref[t] for t in tasks]
    old = [old_ref[t] for t in tasks]
    new = [new_ref[t] for t in tasks]
    zero = jnp.int32(0)
    start, rank = [], []
    for t in tasks:
        at, before = zero, zero
        for u in range(t):
            at = at + jnp.where(old[u] == old[t], count[u], 0)
            before = before + jnp.where(new[u] == new[t], 1, 0)
        start.append(at)
        rank.append(before)
    copies = []
    for k, out in enumerate((kv0_ref, kv1_ref, kv2_ref, kv3_ref)):
        first = zero
        for t in tasks:
            goes = (old[t] == group) & (new[t] == (group + k) % GROUPS)
            first = jnp.where(goes, start[t], first)
        first_ref[k] = first
        for i, ref in enumerate((k_ref, v_ref)):
            copies.append(
                pltpu.make_async_copy(ref.at[pl.ds(first, HALF)], out.at[i], sem.at[2 * k + i])
            )
            copies[-1].start()
    amounts = []
    for r, head in enumerate((head0_ref, head1_ref)):
        came, amount, base = zero, zero, zero
        for t in tasks:
            mine = (new[t] == group) & (rank[t] == r)
            came = jnp.where(mine, (group - old[t] + GROUPS) % GROUPS, came)
            amount = jnp.where(mine, count[t], amount)
            base = jnp.where(mine, old[t] * SLOTS + start[t], base)
        came_ref[r] = came
        amounts.append(amount)
        head[0], head[1], head[2] = z, y, core
        for j in range(2):
            sample = 2 * core + j
            there = sample < amount
            slot = jnp.where(there, base + sample, 0)
            head[3 + j] = jnp.where(there, image_ref[slot], IMG)
            text = jnp.where(there, text_ref[slot], 0)
            head[5 + 2 * j] = text - d * ROWS
            head[6 + 2 * j] = text - (d + 1 - 2 * core) * ROWS
    for slot in range(SLOTS):
        second = jnp.where(slot >= amounts[0], 1, 0)
        j = slot - second * amounts[0]
        at = jnp.where(j // 2 == core, 0, 4) + 2 * second + j % 2
        index_ref[slot] = jnp.where(slot < amounts[0] + amounts[1], at, -1)
    for copy in copies:
        copy.wait()


def pack(counts, old_group, new_group, text_len, image_len, keys, values):
    smem = pl.BlockSpec(memory_space=pltpu.SMEM)
    vmem = pl.BlockSpec(memory_space=pltpu.VMEM)
    kv = jax.ShapeDtypeStruct((2, HALF, KEYS, WIDTH), jnp.bfloat16)
    ints = [jax.ShapeDtypeStruct((n,), jnp.int32) for n in (4, 2, 9, 9, 8)]
    return pl.pallas_call(
        pack_kernel,
        out_shape=(kv,) * 4 + tuple(ints),
        in_specs=[smem] * 5 + [pl.BlockSpec(memory_space=pltpu.HBM)] * 2,
        out_specs=(vmem,) * 4 + (smem,) * 5,
        scratch_shapes=[pltpu.SemaphoreType.DMA((8,))],
        cost_estimate=pl.CostEstimate(flops=1_000_000, bytes_accessed=2_000_000, transcendentals=0),
    )(counts, old_group, new_group, text_len, image_len, keys, values)


def choose_kernel(came_ref, kv0_ref, kv1_ref, kv2_ref, kv3_ref, mine_ref, send_ref, sem):
    core = lax.axis_index("seq") % CORES
    for r in range(2):
        for k, ref in enumerate((kv0_ref, kv1_ref, kv2_ref, kv3_ref)):

            @pl.when(came_ref[r] == k)
            def _():
                for side, (at, out) in enumerate(((2 * core, mine_ref), (2 - 2 * core, send_ref))):
                    pltpu.make_async_copy(
                        ref.at[:, pl.ds(at, 2)], out.at[r], sem.at[r, side]
                    ).start()

    for r in range(2):
        for side, out in enumerate((mine_ref, send_ref)):
            pltpu.make_async_copy(kv0_ref.at[:, pl.ds(0, 2)], out.at[r], sem.at[r, side]).wait()


def choose(came, parts):
    out = jax.ShapeDtypeStruct((2, 2, 2, KEYS, WIDTH), jnp.bfloat16)
    return pl.pallas_call(
        choose_kernel,
        out_shape=(out, out),
        in_specs=[pl.BlockSpec(memory_space=pltpu.SMEM)] + [pl.BlockSpec(memory_space=pl.ANY)] * 4,
        out_specs=(pl.BlockSpec(memory_space=pltpu.VMEM),) * 2,
        scratch_shapes=[pltpu.SemaphoreType.DMA((2, 2))],
        compiler_params=pltpu.CompilerParams(vmem_limit_bytes=4 * 2**20),
        cost_estimate=pl.CostEstimate(flops=1_000_000, bytes_accessed=1_000_000, transcendentals=0),
    )(came, *parts)


def spread_kernel(part, first_ref, x_ref, o0_ref, o1_ref, o2_ref, o3_ref, sem):
    copies = [
        pltpu.make_async_copy(
            x_ref.at[pl.ds(first_ref[k], HALF), pl.ds(part * PART, PART)], out, sem.at[k]
        )
        for k, out in enumerate((o0_ref, o1_ref, o2_ref, o3_ref))
    ]
    for copy in copies:
        copy.start()
    for copy in copies:
        copy.wait()


def spread(part, first, tokens):
    out = jax.ShapeDtypeStruct((HALF, PART, WIDTH), jnp.bfloat16)
    return pl.pallas_call(
        functools.partial(spread_kernel, part),
        out_shape=(out,) * 4,
        in_specs=[pl.BlockSpec(memory_space=pltpu.SMEM), pl.BlockSpec(memory_space=pltpu.HBM)],
        out_specs=(pl.BlockSpec(memory_space=pltpu.VMEM),) * 4,
        scratch_shapes=[pltpu.SemaphoreType.DMA((4,))],
        compiler_params=pltpu.CompilerParams(vmem_limit_bytes=6 * 2**20),
        cost_estimate=pl.CostEstimate(flops=1_000_000, bytes_accessed=4_000_000, transcendentals=0),
    )(first, tokens)


def project_kernel(
    came_ref, head_ref, x0_ref, x1_ref, x2_ref, x3_ref, w_ref, mine_ref, send_ref, x, normal, sem,
):
    core = head_ref[2]
    for r in range(2):
        for k, ref in enumerate((x0_ref, x1_ref, x2_ref, x3_ref)):

            @pl.when(came_ref[r] == k)
            def _():
                for side, at in ((0, 2 * core), (1, 2 - 2 * core)):
                    pltpu.make_async_copy(
                        ref.at[pl.ds(at, 2)], x.at[side, pl.ds(2 * r, 2)], sem.at[r, side]
                    ).start()

    for side in (0, 1):
        side = 1 - side
        for r in range(2):
            pltpu.make_async_copy(
                x0_ref.at[pl.ds(0, 2)], x.at[side, pl.ds(2 * r, 2)], sem.at[r, side]
            ).wait()
        values = x[side].reshape(4 * PART, WIDTH).astype(jnp.float32)
        centred = values - jnp.mean(values, axis=-1, keepdims=True)
        variance = jnp.mean(centred * centred, axis=-1, keepdims=True)
        normal[side] = (centred * lax.rsqrt(variance + norm_eps)).astype(jnp.bfloat16)
    for n in range(8):
        cols = slice(n * 256, (n + 1) * 256)
        both = normal[...].reshape(8 * PART, WIDTH)
        out = jnp.dot(both, w_ref[:, cols], preferred_element_type=jnp.float32)
        out = (out * HEAD_DIM ** (-0.5)).astype(jnp.bfloat16).reshape(2, 4, PART, 256)
        mine_ref[:, :, cols] = out[0]
        send_ref[:, :, cols] = out[1]


def project(came, head, parts, w_query):
    smem = pl.BlockSpec(memory_space=pltpu.SMEM)
    vmem = pl.BlockSpec(memory_space=pltpu.VMEM)
    out = jax.ShapeDtypeStruct((4, PART, WIDTH), jnp.bfloat16)
    return pl.pallas_call(
        project_kernel,
        out_shape=(out, out),
        in_specs=[smem, smem] + [pl.BlockSpec(memory_space=pl.ANY)] * 4 + [vmem],
        out_specs=(vmem, vmem),
        scratch_shapes=[
            pltpu.VMEM((2, 4, PART, WIDTH), jnp.bfloat16),
            pltpu.VMEM((2, 4 * PART, WIDTH), jnp.bfloat16),
            pltpu.SemaphoreType.DMA((2, 2)),
        ],
        compiler_params=pltpu.CompilerParams(vmem_limit_bytes=16 * 2**20),
        cost_estimate=pl.CostEstimate(
            flops=2_150_000_000, bytes_accessed=12_000_000, transcendentals=0
        ),
    )(came, head, *parts, w_query)


def attend_kernel(
    rank, head_ref, qm0_ref, qm1_ref, qt0_ref, qt1_ref,
    own_ref, prev_ref, next_ref, opa_ref, opb_ref, w_ref, om_ref, ot_ref, ctx,
):
    z, y, core = head_ref[0], head_ref[1], head_ref[2]
    i = lax.broadcasted_iota(jnp.int32, (1, IMG), 1)
    run, which, within = i // 64, (i // 16) & 3, i & 15
    hop = jnp.where(run == 1, 3, jnp.where(run == 2, 1, jnp.where(run == 3, 2, 0)))
    back = 4 - which
    at_z = (z + jnp.where(core == 0, back, hop)) & 3
    at_y = (y + jnp.where(core == 0, hop, back)) & 3
    within = (within & 7) + 8 * jnp.where(within < 8, core, 1 - core)
    key_at = 64 * at_z + 16 * at_y + within
    for j in range(2):
        bias = jnp.where(key_at < head_ref[3 + j], 0.0, masked_score)
        for h in range(HEADS):
            cols = slice(h * HEAD_DIM, (h + 1) * HEAD_DIM)

            def side(kv):
                return jnp.concatenate(
                    [
                        ref[:, kv, j, :, cols].reshape(-1, HEAD_DIM)
                        for ref in (own_ref, prev_ref, next_ref, opa_ref, opb_ref)
                    ],
                    axis=0,
                )

            q = jnp.concatenate(
                [ref[2 * rank + j, :, cols] for ref in (qm0_ref, qm1_ref, qt0_ref, qt1_ref)],
                axis=0,
            )
            scores = lax.dot_general(
                q, side(0), (((1,), (1,)), ((), ())), preferred_element_type=jnp.float32
            )
            scores = scores + bias
            top = jnp.max(scores, axis=-1, keepdims=True)
            probs = jnp.exp(scores - top)
            total = jnp.sum(probs, axis=-1, keepdims=True)
            mixed = jnp.dot(
                probs.astype(jnp.bfloat16), side(1), preferred_element_type=jnp.float32
            )
            ctx[2 * ROWS * j : 2 * ROWS * (j + 1), cols] = (mixed * (1.0 / total)).astype(jnp.bfloat16)

    row = lax.broadcasted_iota(jnp.int32, (ROWS, 1), 0)
    for n in range(8):
        cols = slice(n * 256, (n + 1) * 256)
        out = jnp.dot(ctx[...], w_ref[:, cols], preferred_element_type=jnp.float32)
        for j in range(2):
            for side, ref in ((0, om_ref), (1, ot_ref)):
                at = (2 * j + side) * ROWS
                kept = row < head_ref[5 + 2 * j + side]
                ref[j, :, cols] = jnp.where(kept, out[at : at + ROWS], 0.0).astype(jnp.bfloat16)


def attend(rank, head, queries, pieces, w_out):
    vmem = pl.BlockSpec(memory_space=pltpu.VMEM)
    out = jax.ShapeDtypeStruct((2, ROWS, WIDTH), jnp.bfloat16)
    return pl.pallas_call(
        functools.partial(attend_kernel, rank),
        out_shape=(out, out),
        in_specs=[pl.BlockSpec(memory_space=pltpu.SMEM)] + [vmem] * 10,
        out_specs=(vmem, vmem),
        scratch_shapes=[pltpu.VMEM((4 * ROWS, WIDTH), jnp.bfloat16)],
        compiler_params=pltpu.CompilerParams(vmem_limit_bytes=20 * 2**20),
        cost_estimate=pl.CostEstimate(
            flops=3_500_000_000, bytes_accessed=14_000_000, transcendentals=1_000_000
        ),
    )(head, *queries, *pieces, w_out)


def place_kernel(index_ref, m0_ref, m1_ref, t0_ref, t1_ref, out_ref, zeros, sem):
    zeros[...] = jnp.zeros_like(zeros)
    for slot in range(SLOTS):
        source = index_ref[slot]
        for n, ref in enumerate((m0_ref, m1_ref, t0_ref, t1_ref)):
            for j in range(2):

                @pl.when(source == 2 * n + j)
                def _():
                    pltpu.make_async_copy(ref.at[j], out_ref.at[slot], sem.at[slot]).start()

        @pl.when(source < 0)
        def _():
            pltpu.make_async_copy(zeros, out_ref.at[slot], sem.at[slot]).start()

    for slot in range(SLOTS):
        pltpu.make_async_copy(zeros, out_ref.at[slot], sem.at[slot]).wait()


def place(index, m0, m1, t0, t1):
    return pl.pallas_call(
        place_kernel,
        out_shape=jax.ShapeDtypeStruct((SLOTS, ROWS, WIDTH), jnp.bfloat16),
        in_specs=[pl.BlockSpec(memory_space=pltpu.SMEM)]
        + [pl.BlockSpec(memory_space=pltpu.VMEM)] * 4,
        out_specs=pl.BlockSpec(memory_space=pl.ANY),
        scratch_shapes=[
            pltpu.VMEM((ROWS, WIDTH), jnp.bfloat16),
            pltpu.SemaphoreType.DMA((SLOTS,)),
        ],
        compiler_params=pltpu.CompilerParams(vmem_limit_bytes=8 * 2**20),
        cost_estimate=pl.CostEstimate(
            flops=1_000_000, bytes_accessed=4_000_000, transcendentals=0
        ),
    )(index, m0, m1, t0, t1)


def compute(
    tokens, image_keys, image_values, text_len, image_len, counts, old_group, new_group, w_query, w_out
):
    *kv, first, came, head0, head1, index = pack(
        counts, old_group, new_group, text_len, image_len, image_keys, image_values
    )

    for k in (1, 3, 2):
        kv[k] = move_group(kv[k], k)
    parts = []
    for part in range(2):
        x = list(spread(part, first, tokens))
        for k in (1, 3, 2):
            x[k] = move_group(x[k], k)
        parts.append(x)

    kv_mine, kv_send = choose(came, kv)
    kv_theirs = move_seq(kv_send, "swap")
    block = [jnp.concatenate([kv_mine[r], kv_theirs[r]], axis=2) for r in range(2)]

    pieces = []
    for r in range(2):
        near = [block[r]]
        for k in (1, 2, 3):
            near.append(move_seq(block[r], "near", k))
        own = jnp.stack(near)
        prev = move_seq(own, "far", 1)
        after = move_seq(own, "far", 3)
        opa = move_seq(prev[:2], "far", 1)
        opb = move_seq(after[2:], "far", 3)
        pieces.append((own, prev, after, opa, opb))

    mine, theirs = [], []
    for part in range(2):
        q_mine, q_send = project(came, head0, parts[part], w_query)
        mine.append(q_mine)
        theirs.append(move_seq(q_send, "swap"))

    done = []
    for r, head in enumerate((head0, head1)):
        out_mine, out_send = attend(r, head, mine + theirs, pieces[r], w_out)
        done.append((out_mine, move_seq(out_send, "swap")))
    return place(index, done[0][0], done[1][0], done[0][1], done[1][1])


def solution(mesh):
    split = P("group", "seq", None)
    return jax.shard_map(
        compute,
        mesh=mesh,
        in_specs=(split,) * 3 + (P(),) * 7,
        out_specs=split,
        check_vma=False,
    )
```

time: 119 us -> 108 us (0.908)
  Pallas kernels: 33.7 us -> 24.7 us
  waiting for transfers between devices: 39.5 us -> 32.9 us
  starting transfers between devices: 38.6 us -> 41.5 us
  local copies, waits for them, and re-layouts: 5.79 us -> 7.59 us
    ppermute x18 -> x19, waiting for transfers between devices: 37.2 us -> 11 us  [move_seq(): return lax.ppermute(a, 'seq', seq_moves(phase, k))]
    ppermute x6 -> x9, waiting for transfers between devices: 2.33 us -> 22 us  [move_group(): lax.ppermute(a, 'group', [(g, (g + k) % GROUPS) for g in range(GROUPS)])]
    pallas_call x2 -> x4, Pallas kernels: 13.8 us -> 9 us  [the longest x2 7.54 us: project(): pl.pallas_call(project_kernel, out_shape=(out, out), in_specs=[smem, smem...]
    unnamed x18 -> x28, local copies, waits for them, and re-layouts: 4.63 us -> 7.4 us
    ppermute x6 -> x9, starting transfers between devices: 8.51 us -> 11.2 us  [move_group(): lax.ppermute(a, 'group', [(g, (g + k) % GROUPS) for g in range(GROUPS)])]
    pallas_call x2, Pallas kernels: 12.2 us -> 9.52 us  [attend(): pl.pallas_call(functools.partial(attend_kernel, rank), out_shape=(out, ou...]
    pallas_call x1, Pallas kernels: 2.59 us -> 0.99 us  [choose(): pl.pallas_call(choose_kernel, out_shape=(out, out), in_specs=[pl.BlockSpe...]
    ppermute x18 -> x19, starting transfers between devices: 30.1 us -> 30.3 us  [move_seq(): return lax.ppermute(a, 'seq', seq_moves(phase, k))]
  transfers between devices with their start and end apart: 24 -> 28, of which waited for: 9 -> 11; matrix products, arithmetic and copies ran while one was open for 1% -> 0% of each run, Pallas kernels for 24% -> 18%
where the time goes in v1:
time: 108 us
  starting transfers between devices  41.5 us (38%)
  waiting for transfers between devices  32.9 us (30%)
  Pallas kernels  24.7 us (23%)
  local copies, waits for them, and re-layouts  7.59 us (7%)
    ppermute x19, starting transfers between devices, move_seq(): return lax.ppermute(a, 'seq', seq_moves(phase, k))  30.3 us
    ppermute x9, waiting for transfers between devices, move_group(): lax.ppermute(a, 'group', [(g, (g + k) % GROUPS) for g in range(GROUPS)])  22 us
    ppermute x9, starting transfers between devices, move_group(): lax.ppermute(a, 'group', [(g, (g + k) % GROUPS) for g in range(GROUPS)])  11.2 us
    ppermute x19, waiting for transfers between devices, move_seq(): return lax.ppermute(a, 'seq', seq_moves(phase, k))  11 us
    pallas_call x2, Pallas kernels, attend(): pl.pallas_call(functools.partial(attend_kernel, rank), out_shape=(out, ou...  9.52 us
    pallas_call x2, Pallas kernels, project(): pl.pallas_call(project_kernel, out_shape=(out, out), in_specs=[smem, smem...  7.54 us
    unnamed x28, local copies, waits for them, and re-layouts  7.4 us
    pallas_call x1, Pallas kernels, pack(): pl.pallas_call(pack_kernel, out_shape=(kv,) * 4 + tuple(ints), in_specs=[...  3.23 us
  transfers between devices with their start and end apart: 28, of which 11 were waited for; matrix products, arithmetic and copies ran while one was open for 0% of the time, Pallas kernels for 18%

profile of v1, /device:TPU:1, one launch (start us, length us, event | category | flops | bytes accessed | tf_op | source)
XLA Modules:
  0.0 107.5 jit_solution(8136441013461627370)
XLA Ops:
  0.0 3.2 %shard_map.100 = (bf16[2,4,8,2048]{3,2,1,0:T(8,128)(2,1)}, bf16[2,4,8,2048]{3,2,1,0:T(8,128)(2,1)}, bf16[2,4,8,2048]{3,2,1,0:T(8,128)(2,1)}, bf16[2,4,8,2048]{3,...) custom-call(s32[6]{0:T(128)} %counts_ref.1, s32[6]{0:T(128)} %old_ref.1, ...), custom_call_target="tpu_custom_call" | custom-call | flops 1000000 | bytes 2000000 | tf_op jit(solution)/shard_map/pallas_call | solution.py:119
  3.2 2.1 %collective-permute-start.8 = (bf16[2,4,8,2048]{3,2,1,0:T(8,128)(2,1)}, bf16[2,4,8,2048]{3,2,1,0:T(8,128)(2,1)S(1)}, u32[]{:S(2)}, u32[]{:S(2)}) collective-permute-start(bf16[2,4,8,2048]{3,2,1,0:T(8,128)(2,1)} %get-tuple-element.49), channel_id=1, source_target_pairs={{0,32},{32,64},{64,96},{96,0},{1,33},{33,65},{65,97},{97,1},{2,34}... | collective-permute-start | bytes 786440 | tf_op jit(solution)/shard_map/ppermute | solution.py:50
  5.3 2.4 %collective-permute-start.9 = (bf16[2,4,8,2048]{3,2,1,0:T(8,128)(2,1)}, bf16[2,4,8,2048]{3,2,1,0:T(8,128)(2,1)S(1)}, u32[]{:S(2)}, u32[]{:S(2)}) collective-permute-start(bf16[2,4,8,2048]{3,2,1,0:T(8,128)(2,1)} %get-tuple-element.50), channel_id=1, source_target_pairs={{0,64},{32,96},{64,0},{96,32},{1,65},{33,97},{65,1},{97,33},{2,66}... | collective-permute-start | bytes 786440 | tf_op jit(solution)/shard_map/ppermute | solution.py:50
  7.7 1.2 %collective-permute-start.10 = (bf16[2,4,8,2048]{3,2,1,0:T(8,128)(2,1)}, bf16[2,4,8,2048]{3,2,1,0:T(8,128)(2,1)S(1)}, u32[]{:S(2)}, u32[]{:S(2)}) collective-permute-start(bf16[2,4,8,2048]{3,2,1,0:T(8,128)(2,1)} %get-tuple-element.51), channel_id=1, source_target_pairs={{0,96},{32,0},{64,32},{96,64},{1,97},{33,1},{65,33},{97,65},{2,98}... | collective-permute-start | bytes 786440 | tf_op jit(solution)/shard_map/ppermute | solution.py:50
  8.9 1.6 %copy-done.1 = bf16[8,64,2048]{2,1,0:T(8,128)(2,1)S(1)} copy-done((bf16[8,64,2048]{2,1,0:T(8,128)(2,1)S(1)}, bf16[8,64,2048]{2,1,0:T(8,128)(2,1)}, u32[]{:S(2)}) %copy-start.1) | copy-done | bytes 2097176
  13.1 6.2 %collective-permute-done.9.kv2_ref = bf16[2,4,8,2048]{3,2,1,0:T(8,128)(2,1)S(1)} collective-permute-done((bf16[2,4,8,2048]{3,2,1,0:T(8,128)(2,1)}, bf16[2,4,8,2048]{3,2,1,0:T(8,128)(2,1)S(1)}, u32[]{:S(2)}, u32[]{:S(2)}) %collective-permute-start.9) | collective-permute-done | bytes 262176 | tf_op jit(solution)/shard_map/ppermute | solution.py:50
  22.3 2.4 %collective-permute-start.11 = (bf16[2,2,2,8,2048]{4,3,2,1,0:T(8,128)(2,1)S(1)}, bf16[2,2,2,8,2048]{4,3,2,1,0:T(8,128)(2,1)S(1)}, u32[]{:S(2)}, u32[]{:S(2)}) collective-permute-start(bf16[2,2,2,8,2048]{4,3,2,1,0:T(8,128)(2,1)S(1)} %get-tuple-element.53), channel_id=1, source_target_pairs={{0,1},{1,0},{2,3},{3,2},{4,5},{5,4},{6,7},{7,6},{8,9},{9,8},{10,11... | collective-permute-start | bytes 786440 | tf_op jit(solution)/shard_map/ppermute | solution.py:46
  24.7 1.1 %collective-permute-done.11 = bf16[2,2,2,8,2048]{4,3,2,1,0:T(8,128)(2,1)S(1)} collective-permute-done((bf16[2,2,2,8,2048]{4,3,2,1,0:T(8,128)(2,1)S(1)}, bf16[2,2,2,8,2048]{4,3,2,1,0:T(8,128)(2,1)S(1)}, u32[]{:S(2)}, u32[]{:S(2)}) %collective-permute-start.11) | collective-permute-done | bytes 262176 | tf_op jit(solution)/shard_map/ppermute | solution.py:46
  25.9 2.8 %collective-permute-start.14 = (bf16[2,2,16,2048]{3,2,1,0:T(8,128)(2,1)S(1)}, bf16[2,2,16,2048]{3,2,1,0:T(8,128)(2,1)S(1)}, u32[]{:S(2)}, u32[]{:S(2)}) collective-permute-start(bf16[2,2,16,2048]{3,2,1,0:T(8,128)(2,1)S(1)} %get-tuple-element.66), channel_id=1, source_target_pairs={{0,24},{1,7},{2,26},{3,1},{4,28},{5,3},{6,30},{7,5},{8,0},{9,15},{... | collective-permute-start | bytes 786440 | tf_op jit(solution)/shard_map/ppermute | solution.py:46
  29.8 2.6 %collective-permute-done.x1_ref = bf16[4,32,2048]{2,1,0:T(8,128)(2,1)S(1)} collective-permute-done((bf16[4,32,2048]{2,1,0:T(8,128)(2,1)S(1)}, bf16[4,32,2048]{2,1,0:T(8,128)(2,1)S(1)}, u32[]{:S(2)}, u32[]{:S(2)}) %collective-permute-start) | collective-permute-done | bytes 524320 | tf_op jit(solution)/shard_map/ppermute | solution.py:50
  32.4 2.5 %collective-permute-done.14 = bf16[2,2,16,2048]{3,2,1,0:T(8,128)(2,1)S(1)} collective-permute-done((bf16[2,2,16,2048]{3,2,1,0:T(8,128)(2,1)S(1)}, bf16[2,2,16,2048]{3,2,1,0:T(8,128)(2,1)S(1)}, u32[]{:S(2)}, u32[]{:S(2)}) %collective-permute-start.14) | collective-permute-done | bytes 262176 | tf_op jit(solution)/shard_map/ppermute | solution.py:46
  34.9 3.4 %collective-permute-start.21 = (bf16[2,2,16,2048]{3,2,1,0:T(8,128)(2,1)S(1)}, bf16[2,2,16,2048]{3,2,1,0:T(8,128)(2,1)S(1)}, u32[]{:S(2)}, u32[]{:S(2)}) collective-permute-start(bf16[2,2,16,2048]{3,2,1,0:T(8,128)(2,1)S(1)} %get-tuple-element.60), channel_id=1, source_target_pairs={{0,24},{1,7},{2,26},{3,1},{4,28},{5,3},{6,30},{7,5},{8,0},{9,15},{... | collective-permute-start | bytes 786440 | tf_op jit(solution)/shard_map/ppermute | solution.py:46
  38.9 1.6 %copy-done.2 = bf16[8,64,2048]{2,1,0:T(8,128)(2,1)S(1)} copy-done((bf16[8,64,2048]{2,1,0:T(8,128)(2,1)S(1)}, bf16[8,64,2048]{2,1,0:T(8,128)(2,1)}, u32[]{:S(2)}) %copy-start.2) | copy-done | bytes 2097176
  42.7 1.7 %collective-permute-done.21 = bf16[2,2,16,2048]{3,2,1,0:T(8,128)(2,1)S(1)} collective-permute-done((bf16[2,2,16,2048]{3,2,1,0:T(8,128)(2,1)S(1)}, bf16[2,2,16,2048]{3,2,1,0:T(8,128)(2,1)S(1)}, u32[]{:S(2)}, u32[]{:S(2)}) %collective-permute-start.21) | collective-permute-done | bytes 262176 | tf_op jit(solution)/shard_map/ppermute | solution.py:46
  44.4 2.6 %collective-permute-start.4 = (bf16[4,32,2048]{2,1,0:T(8,128)(2,1)S(1)}, bf16[4,32,2048]{2,1,0:T(8,128)(2,1)S(1)}, u32[]{:S(2)}, u32[]{:S(2)}) collective-permute-start(bf16[4,32,2048]{2,1,0:T(8,128)(2,1)S(1)} %get-tuple-element.43), channel_id=1, source_target_pairs={{0,64},{32,96},{64,0},{96,32},{1,65},{33,97},{65,1},{97,33},{2,66}... | collective-permute-start | bytes 1572872 | tf_op jit(solution)/shard_map/ppermute | solution.py:50
  47.0 1.5 %collective-permute-start.15 = (bf16[4,2,2,16,2048]{4,3,2,1,0:T(8,128)(2,1)S(1)}, bf16[4,2,2,16,2048]{4,3,2,1,0:T(8,128)(2,1)S(1)}, u32[]{:S(2)}, u32[]{:S(2)}) collective-permute-start(bf16[4,2,2,16,2048]{4,3,2,1,0:T(8,128)(2,1)S(1)} %pad_maximum_fusion.own_ref), channel_id=1, source_target_pairs={{0,2},{1,9},{2,4},{3,11},{4,6},{5,13},{6,0},{7,15},{8,10},{9,17},{... | collective-permute-start | bytes 3145736 | tf_op jit(solution)/shard_map/ppermute | solution.py:46
  48.5 3.4 %collective-permute-start.16 = (bf16[4,2,2,16,2048]{4,3,2,1,0:T(8,128)(2,1)S(1)}, bf16[4,2,2,16,2048]{4,3,2,1,0:T(8,128)(2,1)S(1)}, u32[]{:S(2)}, u32[]{:S(2)}) collective-permute-start(bf16[4,2,2,16,2048]{4,3,2,1,0:T(8,128)(2,1)S(1)} %pad_maximum_fusion.own_ref), channel_id=1, source_target_pairs={{0,6},{1,25},{2,0},{3,27},{4,2},{5,29},{6,4},{7,31},{8,14},{9,1},{... | collective-permute-start | bytes 3145736 | tf_op jit(solution)/shard_map/ppermute | solution.py:46
  52.1 1.8 %collective-permute-done.3.x1_ref = bf16[4,32,2048]{2,1,0:T(8,128)(2,1)S(1)} collective-permute-done((bf16[4,32,2048]{2,1,0:T(8,128)(2,1)S(1)}, bf16[4,32,2048]{2,1,0:T(8,128)(2,1)S(1)}, u32[]{:S(2)}, u32[]{:S(2)}) %collective-permute-start.3) | collective-permute-done | bytes 524320 | tf_op jit(solution)/shard_map/ppermute | solution.py:50
  54.9 11.0 %collective-permute-done.4.x2_ref = bf16[4,32,2048]{2,1,0:T(8,128)(2,1)S(1)} collective-permute-done((bf16[4,32,2048]{2,1,0:T(8,128)(2,1)S(1)}, bf16[4,32,2048]{2,1,0:T(8,128)(2,1)S(1)}, u32[]{:S(2)}, u32[]{:S(2)}) %collective-permute-start.4) | collective-permute-done | bytes 524320 | tf_op jit(solution)/shard_map/ppermute | solution.py:50
  65.9 5.3 %collective-permute-start.23 = (bf16[4,2,2,16,2048]{4,3,2,1,0:T(8,128)(2,1)S(1)}, bf16[4,2,2,16,2048]{4,3,2,1,0:T(8,128)(2,1)S(1)}, u32[]{:S(2)}, u32[]{:S(2)}) collective-permute-start(bf16[4,2,2,16,2048]{4,3,2,1,0:T(8,128)(2,1)S(1)} %pad_maximum_fusion.1.own_ref), channel_id=1, source_target_pairs={{0,6},{1,25},{2,0},{3,27},{4,2},{5,29},{6,4},{7,31},{8,14},{9,1},{... | collective-permute-start | bytes 3145736 | tf_op jit(solution)/shard_map/ppermute | solution.py:46
  72.6 3.7 %shard_map.102 = (bf16[4,32,2048]{2,1,0:T(8,128)(2,1)S(1)}, bf16[4,32,2048]{2,1,0:T(8,128)(2,1)S(1)}) custom-call(s32[2]{0:T(128)S(1)} %copy-done.7, s32[9]{0:T(128)S(1)} %copy-done.4, bf16[4,32,2048]{2,1,0:T(8,128)(2,1)S(1)} %get-tuple-element.36.x0_ref, bf16[4,32,2048]{2,1,0:T(8,128)(2,1)S(1)} %collective-permute-done.x1_ref, ...), custom_call_target="tpu_custom_call" | custom-call | flops 2150000128 | bytes 12000000 | tf_op jit(solution)/shard_map/pallas_call | solution.py:222
  76.3 1.1 collective-permute-start.6
  77.3 3.9 %shard_map.104 = (bf16[4,32,2048]{2,1,0:T(8,128)(2,1)S(1)}, bf16[4,32,2048]{2,1,0:T(8,128)(2,1)S(1)}) custom-call(s32[2]{0:T(128)S(1)} %copy-done.7, s32[9]{0:T(128)S(1)} %copy-done.4, bf16[4,32,2048]{2,1,0:T(8,128)(2,1)S(1)} %get-tuple-element.41.x0_ref, bf16[4,32,2048]{2,1,0:T(8,128)(2,1)S(1)} %collective-permute-done.3.x1_ref, ...), custom_call_target="tpu_custom_call" | custom-call | flops 2150000128 | bytes 12000000 | tf_op jit(solution)/shard_map/pallas_call | solution.py:222
  81.4 1.7 %collective-permute-start.17 = (bf16[2,2,2,16,2048]{4,3,2,1,0:T(8,128)(2,1)S(1)}, bf16[2,2,2,16,2048]{4,3,2,1,0:T(8,128)(2,1)S(1)}, u32[]{:S(2)}, u32[]{:S(2)}) collective-permute-start(bf16[2,2,2,16,2048]{4,3,2,1,0:T(8,128)(2,1)S(1)} %slice.33), channel_id=1, source_target_pairs={{0,2},{1,9},{2,4},{3,11},{4,6},{5,13},{6,0},{7,15},{8,10},{9,17},{... | collective-permute-start | bytes 1572872 | tf_op jit(solution)/shard_map/ppermute | solution.py:46
  83.2 2.2 %collective-permute-start.18 = (bf16[2,2,2,16,2048]{4,3,2,1,0:T(8,128)(2,1)S(1)}, bf16[2,2,2,16,2048]{4,3,2,1,0:T(8,128)(2,1)S(1)}, u32[]{:S(2)}, u32[]{:S(2)}) collective-permute-start(bf16[2,2,2,16,2048]{4,3,2,1,0:T(8,128)(2,1)S(1)} %slice.34), channel_id=1, source_target_pairs={{0,6},{1,25},{2,0},{3,27},{4,2},{5,29},{6,4},{7,31},{8,14},{9,1},{... | collective-permute-start | bytes 1572872 | tf_op jit(solution)/shard_map/ppermute | solution.py:46
  85.5 2.7 %collective-permute-start.25 = (bf16[2,2,2,16,2048]{4,3,2,1,0:T(8,128)(2,1)S(1)}, bf16[2,2,2,16,2048]{4,3,2,1,0:T(8,128)(2,1)S(1)}, u32[]{:S(2)}, u32[]{:S(2)}) collective-permute-start(bf16[2,2,2,16,2048]{4,3,2,1,0:T(8,128)(2,1)S(1)} %slice.37), channel_id=1, source_target_pairs={{0,6},{1,25},{2,0},{3,27},{4,2},{5,29},{6,4},{7,31},{8,14},{9,1},{... | collective-permute-start | bytes 1572872 | tf_op jit(solution)/shard_map/ppermute | solution.py:46
  88.3 3.8 %collective-permute-done.17.opa_ref = bf16[2,2,2,16,2048]{4,3,2,1,0:T(8,128)(2,1)S(1)} collective-permute-done((bf16[2,2,2,16,2048]{4,3,2,1,0:T(8,128)(2,1)S(1)}, bf16[2,2,2,16,2048]{4,3,2,1,0:T(8,128)(2,1)S(1)}, u32[]{:S(2)}, u32[]{:S(2)}) %collective-permute-start.17) | collective-permute-done | bytes 524320 | tf_op jit(solution)/shard_map/ppermute | solution.py:46
  92.1 4.8 %shard_map.106 = (bf16[2,64,2048]{2,1,0:T(8,128)(2,1)S(1)}, bf16[2,64,2048]{2,1,0:T(8,128)(2,1)S(1)}) custom-call(s32[9]{0:T(128)S(1)} %copy-done.5, bf16[4,32,2048]{2,1,0:T(8,128)(2,1)S(1)} %get-tuple-element.40.qm0_ref, bf16[4,32,2048]{2,1,0:T(8,128)(2,1)S(1)} %get-tuple-element.45.qm1_ref, bf16[4,32,2048]{2,1,0:T(8,128)(2,1)S(1)} %collective-permute-done.6.qt0_ref, ...), custom_call_target="tpu_custom_call" | custom-call | flops 3500000000 | bytes 14000000 | tf_op jit(solution)/shard_map/pallas_call | solution.py:296
  96.9 1.4 %collective-permute-start.26 = (bf16[2,64,2048]{2,1,0:T(8,128)(2,1)S(1)}, bf16[2,64,2048]{2,1,0:T(8,128)(2,1)S(1)}, u32[]{:S(2)}, u32[]{:S(2)}) collective-permute-start(bf16[2,64,2048]{2,1,0:T(8,128)(2,1)S(1)} %get-tuple-element.57), channel_id=1, source_target_pairs={{0,1},{1,0},{2,3},{3,2},{4,5},{5,4},{6,7},{7,6},{8,9},{9,8},{10,11... | collective-permute-start | bytes 1572872 | tf_op jit(solution)/shard_map/ppermute | solution.py:46
  98.3 4.8 %shard_map.107 = (bf16[2,64,2048]{2,1,0:T(8,128)(2,1)S(1)}, bf16[2,64,2048]{2,1,0:T(8,128)(2,1)S(1)}) custom-call(s32[9]{0:T(128)S(1)} %copy-done.11, bf16[4,32,2048]{2,1,0:T(8,128)(2,1)S(1)} %get-tuple-element.40.qm0_ref, bf16[4,32,2048]{2,1,0:T(8,128)(2,1)S(1)} %get-tuple-element.45.qm1_ref, bf16[4,32,2048]{2,1,0:T(8,128)(2,1)S(1)} %collective-permute-done.6.qt0_ref, ...), custom_call_target="tpu_custom_call" | custom-call | flops 3500000000 | bytes 14000000 | tf_op jit(solution)/shard_map/pallas_call | solution.py:296
  103.9 1.5 %collective-permute-done.27.t1_ref = bf16[2,64,2048]{2,1,0:T(8,128)(2,1)S(1)} collective-permute-done((bf16[2,64,2048]{2,1,0:T(8,128)(2,1)S(1)}, bf16[2,64,2048]{2,1,0:T(8,128)(2,1)S(1)}, u32[]{:S(2)}, u32[]{:S(2)}) %collective-permute-start.27) | collective-permute-done | bytes 524320 | tf_op jit(solution)/shard_map/ppermute | solution.py:46
  105.4 1.9 %shard_map.108 = bf16[8,64,2048]{2,1,0:T(8,128)(2,1)} custom-call(s32[8]{0:T(128)S(1)} %copy-done.10, bf16[2,64,2048]{2,1,0:T(8,128)(2,1)S(1)} %get-tuple-element.54.m0_ref, bf16[2,64,2048]{2,1,0:T(8,128)(2,1)S(1)} %get-tuple-element.56.m1_ref, bf16[2,64,2048]{2,1,0:T(8,128)(2,1)S(1)} %collective-permute-done.26.t0_ref, ...), custom_call_target="tpu_custom_call" | custom-call | flops 1000000 | bytes 4000000 | tf_op jit(solution)/shard_map/pallas_call | solution.py:329
  (72 shorter events, 13.3 us)
Async XLA Ops:
  3.2 68.0 %copy-start = (bf16[2048,2048]{1,0:T(8,128)(2,1)S(1)}, bf16[2048,2048]{1,0:T(8,128)(2,1)}, u32[]{:S(2)}) copy-start(bf16[2048,2048]{1,0:T(8,128)(2,1)} %w_ref.5) | copy-start | bytes 25165828
  3.2 9.9 %collective-permute-start.8 = (bf16[2,4,8,2048]{3,2,1,0:T(8,128)(2,1)}, bf16[2,4,8,2048]{3,2,1,0:T(8,128)(2,1)S(1)}, u32[]{:S(2)}, u32[]{:S(2)}) collective-permute-start(bf16[2,4,8,2048]{3,2,1,0:T(8,128)(2,1)} %get-tuple-element.49), channel_id=1, source_target_pairs={{0,32},{32,64},{64,96},{96,0},{1,33},{33,65},{65,97},{97,1},{2,34}... | collective-permute-start | bytes 786440 | tf_op jit(solution)/shard_map/ppermute | solution.py:50
  5.3 14.0 %collective-permute-start.9 = (bf16[2,4,8,2048]{3,2,1,0:T(8,128)(2,1)}, bf16[2,4,8,2048]{3,2,1,0:T(8,128)(2,1)S(1)}, u32[]{:S(2)}, u32[]{:S(2)}) collective-permute-start(bf16[2,4,8,2048]{3,2,1,0:T(8,128)(2,1)} %get-tuple-element.50), channel_id=1, source_target_pairs={{0,64},{32,96},{64,0},{96,32},{1,65},{33,97},{65,1},{97,33},{2,66}... | collective-permute-start | bytes 786440 | tf_op jit(solution)/shard_map/ppermute | solution.py:50
  7.7 12.0 %collective-permute-start.10 = (bf16[2,4,8,2048]{3,2,1,0:T(8,128)(2,1)}, bf16[2,4,8,2048]{3,2,1,0:T(8,128)(2,1)S(1)}, u32[]{:S(2)}, u32[]{:S(2)}) collective-permute-start(bf16[2,4,8,2048]{3,2,1,0:T(8,128)(2,1)} %get-tuple-element.51), channel_id=1, source_target_pairs={{0,96},{32,0},{64,32},{96,64},{1,97},{33,1},{65,33},{97,65},{2,98}... | collective-permute-start | bytes 786440 | tf_op jit(solution)/shard_map/ppermute | solution.py:50
  11.8 20.5 %collective-permute-start = (bf16[4,32,2048]{2,1,0:T(8,128)(2,1)S(1)}, bf16[4,32,2048]{2,1,0:T(8,128)(2,1)S(1)}, u32[]{:S(2)}, u32[]{:S(2)}) collective-permute-start(bf16[4,32,2048]{2,1,0:T(8,128)(2,1)S(1)} %get-tuple-element.37), channel_id=1, source_target_pairs={{0,32},{32,64},{64,96},{96,0},{1,33},{33,65},{65,97},{97,1},{2,34}... | collective-permute-start | bytes 1572872 | tf_op jit(solution)/shard_map/ppermute | solution.py:50
  12.2 29.7 %collective-permute-start.1 = (bf16[4,32,2048]{2,1,0:T(8,128)(2,1)S(1)}, bf16[4,32,2048]{2,1,0:T(8,128)(2,1)S(1)}, u32[]{:S(2)}, u32[]{:S(2)}) collective-permute-start(bf16[4,32,2048]{2,1,0:T(8,128)(2,1)S(1)} %get-tuple-element.38), channel_id=1, source_target_pairs={{0,64},{32,96},{64,0},{96,32},{1,65},{33,97},{65,1},{97,33},{2,66}... | collective-permute-start | bytes 1572872 | tf_op jit(solution)/shard_map/ppermute | solution.py:50
  22.3 3.5 %collective-permute-start.11 = (bf16[2,2,2,8,2048]{4,3,2,1,0:T(8,128)(2,1)S(1)}, bf16[2,2,2,8,2048]{4,3,2,1,0:T(8,128)(2,1)S(1)}, u32[]{:S(2)}, u32[]{:S(2)}) collective-permute-start(bf16[2,2,2,8,2048]{4,3,2,1,0:T(8,128)(2,1)S(1)} %get-tuple-element.53), channel_id=1, source_target_pairs={{0,1},{1,0},{2,3},{3,2},{4,5},{5,4},{6,7},{7,6},{8,9},{9,8},{10,11... | collective-permute-start | bytes 786440 | tf_op jit(solution)/shard_map/ppermute | solution.py:46
  25.9 8.9 %collective-permute-start.14 = (bf16[2,2,16,2048]{3,2,1,0:T(8,128)(2,1)S(1)}, bf16[2,2,16,2048]{3,2,1,0:T(8,128)(2,1)S(1)}, u32[]{:S(2)}, u32[]{:S(2)}) collective-permute-start(bf16[2,2,16,2048]{3,2,1,0:T(8,128)(2,1)S(1)} %get-tuple-element.66), channel_id=1, source_target_pairs={{0,24},{1,7},{2,26},{3,1},{4,28},{5,3},{6,30},{7,5},{8,0},{9,15},{... | collective-permute-start | bytes 786440 | tf_op jit(solution)/shard_map/ppermute | solution.py:46
  28.7 9.5 %collective-permute-start.13 = (bf16[2,2,16,2048]{3,2,1,0:T(8,128)(2,1)S(1)}, bf16[2,2,16,2048]{3,2,1,0:T(8,128)(2,1)S(1)}, u32[]{:S(2)}, u32[]{:S(2)}) collective-permute-start(bf16[2,2,16,2048]{3,2,1,0:T(8,128)(2,1)S(1)} %get-tuple-element.66), channel_id=1, source_target_pairs={{0,16},{1,5},{2,18},{3,7},{4,20},{5,1},{6,22},{7,3},{8,24},{9,13},... | collective-permute-start | bytes 786440 | tf_op jit(solution)/shard_map/ppermute | solution.py:46
  29.1 9.5 %collective-permute-start.12 = (bf16[2,2,16,2048]{3,2,1,0:T(8,128)(2,1)S(1)}, bf16[2,2,16,2048]{3,2,1,0:T(8,128)(2,1)S(1)}, u32[]{:S(2)}, u32[]{:S(2)}) collective-permute-start(bf16[2,2,16,2048]{3,2,1,0:T(8,128)(2,1)S(1)} %get-tuple-element.66), channel_id=1, source_target_pairs={{0,8},{1,3},{2,10},{3,5},{4,12},{5,7},{6,14},{7,1},{8,16},{9,11},{... | collective-permute-start | bytes 786440 | tf_op jit(solution)/shard_map/ppermute | solution.py:46
  32.3 19.7 %collective-permute-start.2 = (bf16[4,32,2048]{2,1,0:T(8,128)(2,1)S(1)}, bf16[4,32,2048]{2,1,0:T(8,128)(2,1)S(1)}, u32[]{:S(2)}, u32[]{:S(2)}) collective-permute-start(bf16[4,32,2048]{2,1,0:T(8,128)(2,1)S(1)} %get-tuple-element.39), channel_id=1, source_target_pairs={{0,96},{32,0},{64,32},{96,64},{1,97},{33,1},{65,33},{97,65},{2,98}... | collective-permute-start | bytes 1572872 | tf_op jit(solution)/shard_map/ppermute | solution.py:50
  34.9 9.5 %collective-permute-start.21 = (bf16[2,2,16,2048]{3,2,1,0:T(8,128)(2,1)S(1)}, bf16[2,2,16,2048]{3,2,1,0:T(8,128)(2,1)S(1)}, u32[]{:S(2)}, u32[]{:S(2)}) collective-permute-start(bf16[2,2,16,2048]{3,2,1,0:T(8,128)(2,1)S(1)} %get-tuple-element.60), channel_id=1, source_target_pairs={{0,24},{1,7},{2,26},{3,1},{4,28},{5,3},{6,30},{7,5},{8,0},{9,15},{... | collective-permute-start | bytes 786440 | tf_op jit(solution)/shard_map/ppermute | solution.py:46
  38.3 8.7 %collective-permute-start.20 = (bf16[2,2,16,2048]{3,2,1,0:T(8,128)(2,1)S(1)}, bf16[2,2,16,2048]{3,2,1,0:T(8,128)(2,1)S(1)}, u32[]{:S(2)}, u32[]{:S(2)}) collective-permute-start(bf16[2,2,16,2048]{3,2,1,0:T(8,128)(2,1)S(1)} %get-tuple-element.60), channel_id=1, source_target_pairs={{0,16},{1,5},{2,18},{3,7},{4,20},{5,1},{6,22},{7,3},{8,24},{9,13},... | collective-permute-start | bytes 786440 | tf_op jit(solution)/shard_map/ppermute | solution.py:46
  38.6 9.9 %collective-permute-start.19 = (bf16[2,2,16,2048]{3,2,1,0:T(8,128)(2,1)S(1)}, bf16[2,2,16,2048]{3,2,1,0:T(8,128)(2,1)S(1)}, u32[]{:S(2)}, u32[]{:S(2)}) collective-permute-start(bf16[2,2,16,2048]{3,2,1,0:T(8,128)(2,1)S(1)} %get-tuple-element.60), channel_id=1, source_target_pairs={{0,8},{1,3},{2,10},{3,5},{4,12},{5,7},{6,14},{7,1},{8,16},{9,11},{... | collective-permute-start | bytes 786440 | tf_op jit(solution)/shard_map/ppermute | solution.py:46
  42.0 11.9 %collective-permute-start.3 = (bf16[4,32,2048]{2,1,0:T(8,128)(2,1)S(1)}, bf16[4,32,2048]{2,1,0:T(8,128)(2,1)S(1)}, u32[]{:S(2)}, u32[]{:S(2)}) collective-permute-start(bf16[4,32,2048]{2,1,0:T(8,128)(2,1)S(1)} %get-tuple-element.42), channel_id=1, source_target_pairs={{0,32},{32,64},{64,96},{96,0},{1,33},{33,65},{65,97},{97,1},{2,34}... | collective-permute-start | bytes 1572872 | tf_op jit(solution)/shard_map/ppermute | solution.py:50
  44.4 21.5 %collective-permute-start.4 = (bf16[4,32,2048]{2,1,0:T(8,128)(2,1)S(1)}, bf16[4,32,2048]{2,1,0:T(8,128)(2,1)S(1)}, u32[]{:S(2)}, u32[]{:S(2)}) collective-permute-start(bf16[4,32,2048]{2,1,0:T(8,128)(2,1)S(1)} %get-tuple-element.43), channel_id=1, source_target_pairs={{0,64},{32,96},{64,0},{96,32},{1,65},{33,97},{65,1},{97,33},{2,66}... | collective-permute-start | bytes 1572872 | tf_op jit(solution)/shard_map/ppermute | solution.py:50
  47.0 34.2 %collective-permute-start.15 = (bf16[4,2,2,16,2048]{4,3,2,1,0:T(8,128)(2,1)S(1)}, bf16[4,2,2,16,2048]{4,3,2,1,0:T(8,128)(2,1)S(1)}, u32[]{:S(2)}, u32[]{:S(2)}) collective-permute-start(bf16[4,2,2,16,2048]{4,3,2,1,0:T(8,128)(2,1)S(1)} %pad_maximum_fusion.own_ref), channel_id=1, source_target_pairs={{0,2},{1,9},{2,4},{3,11},{4,6},{5,13},{6,0},{7,15},{8,10},{9,17},{... | collective-permute-start | bytes 3145736 | tf_op jit(solution)/shard_map/ppermute | solution.py:46
  48.5 32.9 %collective-permute-start.16 = (bf16[4,2,2,16,2048]{4,3,2,1,0:T(8,128)(2,1)S(1)}, bf16[4,2,2,16,2048]{4,3,2,1,0:T(8,128)(2,1)S(1)}, u32[]{:S(2)}, u32[]{:S(2)}) collective-permute-start(bf16[4,2,2,16,2048]{4,3,2,1,0:T(8,128)(2,1)S(1)} %pad_maximum_fusion.own_ref), channel_id=1, source_target_pairs={{0,6},{1,25},{2,0},{3,27},{4,2},{5,29},{6,4},{7,31},{8,14},{9,1},{... | collective-permute-start | bytes 3145736 | tf_op jit(solution)/shard_map/ppermute | solution.py:46
  52.0 31.1 %collective-permute-start.22 = (bf16[4,2,2,16,2048]{4,3,2,1,0:T(8,128)(2,1)S(1)}, bf16[4,2,2,16,2048]{4,3,2,1,0:T(8,128)(2,1)S(1)}, u32[]{:S(2)}, u32[]{:S(2)}) collective-permute-start(bf16[4,2,2,16,2048]{4,3,2,1,0:T(8,128)(2,1)S(1)} %pad_maximum_fusion.1.own_ref), channel_id=1, source_target_pairs={{0,2},{1,9},{2,4},{3,11},{4,6},{5,13},{6,0},{7,15},{8,10},{9,17},{... | collective-permute-start | bytes 3145736 | tf_op jit(solution)/shard_map/ppermute | solution.py:46
  53.9 22.4 %collective-permute-start.5 = (bf16[4,32,2048]{2,1,0:T(8,128)(2,1)S(1)}, bf16[4,32,2048]{2,1,0:T(8,128)(2,1)S(1)}, u32[]{:S(2)}, u32[]{:S(2)}) collective-permute-start(bf16[4,32,2048]{2,1,0:T(8,128)(2,1)S(1)} %get-tuple-element.44), channel_id=1, source_target_pairs={{0,96},{32,0},{64,32},{96,64},{1,97},{33,1},{65,33},{97,65},{2,98}... | collective-permute-start | bytes 1572872 | tf_op jit(solution)/shard_map/ppermute | solution.py:50
  65.9 19.5 %collective-permute-start.23 = (bf16[4,2,2,16,2048]{4,3,2,1,0:T(8,128)(2,1)S(1)}, bf16[4,2,2,16,2048]{4,3,2,1,0:T(8,128)(2,1)S(1)}, u32[]{:S(2)}, u32[]{:S(2)}) collective-permute-start(bf16[4,2,2,16,2048]{4,3,2,1,0:T(8,128)(2,1)S(1)} %pad_maximum_fusion.1.own_ref), channel_id=1, source_target_pairs={{0,6},{1,25},{2,0},{3,27},{4,2},{5,29},{6,4},{7,31},{8,14},{9,1},{... | collective-permute-start | bytes 3145736 | tf_op jit(solution)/shard_map/ppermute | solution.py:46
  72.6 19.5 %slice-start = ((s8[8388608]{0:T(1024)(128)(4,1)}), s8[4194304]{0:T(1024)(128)(4,1)S(1)}, s32[]{:S(2)}) async-start(s8[8388608]{0:T(1024)(128)(4,1)} %bitcast.18), calls=%async_computation | async-start | bytes 8388608
  76.3 15.8 %copy-start.5 = (s32[9]{0:T(128)S(1)}, s32[9]{0:T(128)}, u32[]{:S(2)}) copy-start(s32[9]{0:T(128)} %get-tuple-element.33.head_ref) | copy-start | bytes 112
  76.3 9.3 %collective-permute-start.6 = (bf16[4,32,2048]{2,1,0:T(8,128)(2,1)S(1)}, bf16[4,32,2048]{2,1,0:T(8,128)(2,1)S(1)}, u32[]{:S(2)}, u32[]{:S(2)}) collective-permute-start(bf16[4,32,2048]{2,1,0:T(8,128)(2,1)S(1)} %get-tuple-element.46), channel_id=1, source_target_pairs={{0,1},{1,0},{2,3},{3,2},{4,5},{5,4},{6,7},{7,6},{8,9},{9,8},{10,11... | collective-permute-start | bytes 1572872 | tf_op jit(solution)/shard_map/ppermute | solution.py:46
  81.2 7.1 %collective-permute-start.7 = (bf16[4,32,2048]{2,1,0:T(8,128)(2,1)S(1)}, bf16[4,32,2048]{2,1,0:T(8,128)(2,1)S(1)}, u32[]{:S(2)}, u32[]{:S(2)}) collective-permute-start(bf16[4,32,2048]{2,1,0:T(8,128)(2,1)S(1)} %get-tuple-element.47), channel_id=1, source_target_pairs={{0,1},{1,0},{2,3},{3,2},{4,5},{5,4},{6,7},{7,6},{8,9},{9,8},{10,11... | collective-permute-start | bytes 1572872 | tf_op jit(solution)/shard_map/ppermute | solution.py:46
  81.4 10.7 %collective-permute-start.17 = (bf16[2,2,2,16,2048]{4,3,2,1,0:T(8,128)(2,1)S(1)}, bf16[2,2,2,16,2048]{4,3,2,1,0:T(8,128)(2,1)S(1)}, u32[]{:S(2)}, u32[]{:S(2)}) collective-permute-start(bf16[2,2,2,16,2048]{4,3,2,1,0:T(8,128)(2,1)S(1)} %slice.33), channel_id=1, source_target_pairs={{0,2},{1,9},{2,4},{3,11},{4,6},{5,13},{6,0},{7,15},{8,10},{9,17},{... | collective-permute-start | bytes 1572872 | tf_op jit(solution)/shard_map/ppermute | solution.py:46
  83.1 15.1 %copy-start.11 = (s32[9]{0:T(128)S(1)}, s32[9]{0:T(128)}, u32[]{:S(2)}) copy-start(s32[9]{0:T(128)} %get-tuple-element.55.head_ref) | copy-start | bytes 112
  83.2 8.9 %collective-permute-start.18 = (bf16[2,2,2,16,2048]{4,3,2,1,0:T(8,128)(2,1)S(1)}, bf16[2,2,2,16,2048]{4,3,2,1,0:T(8,128)(2,1)S(1)}, u32[]{:S(2)}, u32[]{:S(2)}) collective-permute-start(bf16[2,2,2,16,2048]{4,3,2,1,0:T(8,128)(2,1)S(1)} %slice.34), channel_id=1, source_target_pairs={{0,6},{1,25},{2,0},{3,27},{4,2},{5,29},{6,4},{7,31},{8,14},{9,1},{... | collective-permute-start | bytes 1572872 | tf_op jit(solution)/shard_map/ppermute | solution.py:46
  85.4 12.9 %collective-permute-start.24 = (bf16[2,2,2,16,2048]{4,3,2,1,0:T(8,128)(2,1)S(1)}, bf16[2,2,2,16,2048]{4,3,2,1,0:T(8,128)(2,1)S(1)}, u32[]{:S(2)}, u32[]{:S(2)}) collective-permute-start(bf16[2,2,2,16,2048]{4,3,2,1,0:T(8,128)(2,1)S(1)} %slice.36), channel_id=1, source_target_pairs={{0,2},{1,9},{2,4},{3,11},{4,6},{5,13},{6,0},{7,15},{8,10},{9,17},{... | collective-permute-start | bytes 1572872 | tf_op jit(solution)/shard_map/ppermute | solution.py:46
  85.5 12.7 %collective-permute-start.25 = (bf16[2,2,2,16,2048]{4,3,2,1,0:T(8,128)(2,1)S(1)}, bf16[2,2,2,16,2048]{4,3,2,1,0:T(8,128)(2,1)S(1)}, u32[]{:S(2)}, u32[]{:S(2)}) collective-permute-start(bf16[2,2,2,16,2048]{4,3,2,1,0:T(8,128)(2,1)S(1)} %slice.37), channel_id=1, source_target_pairs={{0,6},{1,25},{2,0},{3,27},{4,2},{5,29},{6,4},{7,31},{8,14},{9,1},{... | collective-permute-start | bytes 1572872 | tf_op jit(solution)/shard_map/ppermute | solution.py:46
  96.9 7.0 %collective-permute-start.26 = (bf16[2,64,2048]{2,1,0:T(8,128)(2,1)S(1)}, bf16[2,64,2048]{2,1,0:T(8,128)(2,1)S(1)}, u32[]{:S(2)}, u32[]{:S(2)}) collective-permute-start(bf16[2,64,2048]{2,1,0:T(8,128)(2,1)S(1)} %get-tuple-element.57), channel_id=1, source_target_pairs={{0,1},{1,0},{2,3},{3,2},{4,5},{5,4},{6,7},{7,6},{8,9},{9,8},{10,11... | collective-permute-start | bytes 1572872 | tf_op jit(solution)/shard_map/ppermute | solution.py:46
  103.1 2.4 %collective-permute-start.27 = (bf16[2,64,2048]{2,1,0:T(8,128)(2,1)S(1)}, bf16[2,64,2048]{2,1,0:T(8,128)(2,1)S(1)}, u32[]{:S(2)}, u32[]{:S(2)}) collective-permute-start(bf16[2,64,2048]{2,1,0:T(8,128)(2,1)S(1)} %get-tuple-element.58), channel_id=1, source_target_pairs={{0,1},{1,0},{2,3},{3,2},{4,5},{5,4},{6,7},{7,6},{8,9},{9,8},{10,11... | collective-permute-start | bytes 1572872 | tf_op jit(solution)/shard_map/ppermute | solution.py:46
  (10 other events, 30.7 us)

commit v2 on v1

--- a/solution.py
+++ b/solution.py
@@ -122,6 +122,7 @@
         in_specs=[smem] * 5 + [pl.BlockSpec(memory_space=pltpu.HBM)] * 2,
         out_specs=(vmem,) * 4 + (smem,) * 5,
         scratch_shapes=[pltpu.SemaphoreType.DMA((8,))],
+        compiler_params=pltpu.CompilerParams(vmem_limit_bytes=6 * 2**20),
         cost_estimate=pl.CostEstimate(flops=1_000_000, bytes_accessed=2_000_000, transcendentals=0),
     )(counts, old_group, new_group, text_len, image_len, keys, values)
 
@@ -156,63 +157,50 @@
     )(came, *parts)
 
 
-def spread_kernel(part, first_ref, x_ref, o0_ref, o1_ref, o2_ref, o3_ref, sem):
-    copies = [
+def scaled_queries(normal, w_ref, n):
+    out = jnp.dot(normal, w_ref[:, n * 256 : (n + 1) * 256], preferred_element_type=jnp.float32)
+    return (out * HEAD_DIM ** (-0.5)).astype(jnp.bfloat16)
+
+
+def normalized(x):
+    values = x.reshape(-1, WIDTH).astype(jnp.float32)
+    centred = values - jnp.mean(values, axis=-1, keepdims=True)
+    variance = jnp.mean(centred * centred, axis=-1, keepdims=True)
+    return (centred * lax.rsqrt(variance + norm_eps)).astype(jnp.bfloat16)
+
+
+def start_picks(came_ref, core, parts, mine, send, sem):
+    for r in range(2):
+        for k, ref in enumerate(parts):
+
+            @pl.when(came_ref[r] == k)
+            def _():
+                for side, (at, out) in enumerate(((2 * core, mine), (2 - 2 * core, send))):
+                    pltpu.make_async_copy(
+                        ref.at[pl.ds(at, 2)], out.at[pl.ds(2 * r, 2)], sem.at[r, side]
+                    ).start()
+
+
+def wait_picks(parts, side, out, sem):
+    for r in range(2):
         pltpu.make_async_copy(
-            x_ref.at[pl.ds(first_ref[k], HALF), pl.ds(part * PART, PART)], out, sem.at[k]
-        )
-        for k, out in enumerate((o0_ref, o1_ref, o2_ref, o3_ref))
-    ]
-    for copy in copies:
-        copy.start()
-    for copy in copies:
-        copy.wait()
-
-
-def spread(part, first, tokens):
-    out = jax.ShapeDtypeStruct((HALF, PART, WIDTH), jnp.bfloat16)
-    return pl.pallas_call(
-        functools.partial(spread_kernel, part),
-        out_shape=(out,) * 4,
-        in_specs=[pl.BlockSpec(memory_space=pltpu.SMEM), pl.BlockSpec(memory_space=pltpu.HBM)],
-        out_specs=(pl.BlockSpec(memory_space=pltpu.VMEM),) * 4,
-        scratch_shapes=[pltpu.SemaphoreType.DMA((4,))],
-        compiler_params=pltpu.CompilerParams(vmem_limit_bytes=6 * 2**20),
-        cost_estimate=pl.CostEstimate(flops=1_000_000, bytes_accessed=4_000_000, transcendentals=0),
-    )(first, tokens)
+            parts[0].at[pl.ds(0, 2)], out.at[pl.ds(2 * r, 2)], sem.at[r, side]
+        ).wait()
 
 
 def project_kernel(
     came_ref, head_ref, x0_ref, x1_ref, x2_ref, x3_ref, w_ref, mine_ref, send_ref, x, normal, sem,
 ):
-    core = head_ref[2]
-    for r in range(2):
-        for k, ref in enumerate((x0_ref, x1_ref, x2_ref, x3_ref)):
-
-            @pl.when(came_ref[r] == k)
-            def _():
-                for side, at in ((0, 2 * core), (1, 2 - 2 * core)):
-                    pltpu.make_async_copy(
-                        ref.at[pl.ds(at, 2)], x.at[side, pl.ds(2 * r, 2)], sem.at[r, side]
-                    ).start()
-
-    for side in (0, 1):
-        side = 1 - side
-        for r in range(2):
-            pltpu.make_async_copy(
-                x0_ref.at[pl.ds(0, 2)], x.at[side, pl.ds(2 * r, 2)], sem.at[r, side]
-            ).wait()
-        values = x[side].reshape(4 * PART, WIDTH).astype(jnp.float32)
-        centred = values - jnp.mean(values, axis=-1, keepdims=True)
-        variance = jnp.mean(centred * centred, axis=-1, keepdims=True)
-        normal[side] = (centred * lax.rsqrt(variance + norm_eps)).astype(jnp.bfloat16)
+    parts = (x0_ref, x1_ref, x2_ref, x3_ref)
+    start_picks(came_ref, head_ref[2], parts, x.at[0], x.at[1], sem)
+    for side in range(2):
+        wait_picks(parts, side, x.at[side], sem)
+        normal[side] = normalized(x[side])
     for n in range(8):
-        cols = slice(n * 256, (n + 1) * 256)
         both = normal[...].reshape(8 * PART, WIDTH)
-        out = jnp.dot(both, w_ref[:, cols], preferred_element_type=jnp.float32)
-        out = (out * HEAD_DIM ** (-0.5)).astype(jnp.bfloat16).reshape(2, 4, PART, 256)
-        mine_ref[:, :, cols] = out[0]
-        send_ref[:, :, cols] = out[1]
+        out = scaled_queries(both, w_ref, n).reshape(2, 4, PART, 256)
+        mine_ref[:, :, n * 256 : (n + 1) * 256] = out[0]
+        send_ref[:, :, n * 256 : (n + 1) * 256] = out[1]
 
 
 def project(came, head, parts, w_query):
@@ -234,6 +222,94 @@
             flops=2_150_000_000, bytes_accessed=12_000_000, transcendentals=0
         ),
     )(came, head, *parts, w_query)
+
+
+def early_kernel(
+    first_ref, x_ref, w_hbm, t0_ref, t1_ref, t2_ref, t3_ref, o0_ref, o1_ref, o2_ref, o3_ref,
+    x, normal, queries, w_ref, sem, w_sem, t_sem,
+):
+    raw = [
+        pltpu.make_async_copy(
+            x_ref.at[pl.ds(first_ref[k], HALF), pl.ds(0, PART)], out, t_sem.at[k]
+        )
+        for k, out in enumerate((t0_ref, t1_ref, t2_ref, t3_ref))
+    ]
+    blocks = [
+        pltpu.make_async_copy(
+            w_hbm.at[:, pl.ds(512 * i, 512)], w_ref.at[:, pl.ds(512 * i, 512)], w_sem.at[i]
+        )
+        for i in range(4)
+    ]
+    copies = [
+        pltpu.make_async_copy(
+            x_ref.at[pl.ds(4 * i, 4), pl.ds(PART, PART)], x.at[pl.ds(4 * i, 4)], sem.at[i]
+        )
+        for i in range(2)
+    ]
+    for copy in copies + blocks + raw:
+        copy.start()
+    for i, copy in enumerate(copies):
+        copy.wait()
+        normal[4 * PART * i : 4 * PART * (i + 1)] = normalized(x[4 * i : 4 * i + 4])
+    for n in range(8):
+        if n % 2 == 0:
+            blocks[n // 2].wait()
+        out = scaled_queries(normal[...], w_ref, n)
+        queries[:, :, n * 256 : (n + 1) * 256] = out.reshape(SLOTS, PART, 256)
+    for k, out in enumerate((o0_ref, o1_ref, o2_ref, o3_ref)):
+        out[...] = queries[pl.ds(first_ref[k], HALF)]
+    for copy in raw:
+        copy.wait()
+
+
+def early(first, tokens, w_query):
+    vmem = pl.BlockSpec(memory_space=pltpu.VMEM)
+    out = jax.ShapeDtypeStruct((HALF, PART, WIDTH), jnp.bfloat16)
+    return pl.pallas_call(
+        early_kernel,
+        out_shape=(out,) * 8,
+        in_specs=[
+            pl.BlockSpec(memory_space=pltpu.SMEM),
+            pl.BlockSpec(memory_space=pltpu.HBM),
+            pl.BlockSpec(memory_space=pltpu.HBM),
+        ],
+        out_specs=(vmem,) * 8,
+        scratch_shapes=[
+            pltpu.VMEM((SLOTS, PART, WIDTH), jnp.bfloat16),
+            pltpu.VMEM((SLOTS * PART, WIDTH), jnp.bfloat16),
+            pltpu.VMEM((SLOTS, PART, WIDTH), jnp.bfloat16),
+            pltpu.VMEM((WIDTH, WIDTH), jnp.bfloat16),
+            pltpu.SemaphoreType.DMA((2,)),
+            pltpu.SemaphoreType.DMA((4,)),
+            pltpu.SemaphoreType.DMA((4,)),
+        ],
+        compiler_params=pltpu.CompilerParams(vmem_limit_bytes=20 * 2**20),
+        cost_estimate=pl.CostEstimate(
+            flops=2_150_000_000, bytes_accessed=12_000_000, transcendentals=0
+        ),
+    )(first, tokens, w_query)
+
+
+def late_kernel(came_ref, head_ref, x0_ref, x1_ref, x2_ref, x3_ref, mine_ref, send_ref, sem):
+    parts = (x0_ref, x1_ref, x2_ref, x3_ref)
+    start_picks(came_ref, head_ref[2], parts, mine_ref, send_ref, sem)
+    wait_picks(parts, 0, mine_ref, sem)
+    wait_picks(parts, 1, send_ref, sem)
+
+
+def late(came, head, parts):
+    smem = pl.BlockSpec(memory_space=pltpu.SMEM)
+    vmem = pl.BlockSpec(memory_space=pltpu.VMEM)
+    out = jax.ShapeDtypeStruct((4, PART, WIDTH), jnp.bfloat16)
+    return pl.pallas_call(
+        late_kernel,
+        out_shape=(out, out),
+        in_specs=[smem, smem] + [pl.BlockSpec(memory_space=pl.ANY)] * 4,
+        out_specs=(vmem, vmem),
+        scratch_shapes=[pltpu.SemaphoreType.DMA((2, 2))],
+        compiler_params=pltpu.CompilerParams(vmem_limit_bytes=4 * 2**20),
+        cost_estimate=pl.CostEstimate(flops=1_000_000, bytes_accessed=2_000_000, transcendentals=0),
+    )(came, head, *parts)
 
 
 def attend_kernel(
@@ -346,6 +422,11 @@
 def compute(
     tokens, image_keys, image_values, text_len, image_len, counts, old_group, new_group, w_query, w_out
 ):
+    small = (counts, old_group, new_group, text_len, image_len, image_keys, image_values, tokens)
+    counts, old_group, new_group, text_len, image_len, image_keys, image_values, tokens = (
+        pltpu.with_memory_space_constraint(a, pltpu.HBM) for a in small
+    )
+    w_far = pltpu.with_memory_space_constraint(w_query, pltpu.HBM)
     *kv, first, came, head0, head1, index = pack(
         counts, old_group, new_group, text_len, image_len, image_keys, image_values
     )
@@ -353,8 +434,9 @@
     for k in (1, 3, 2):
         kv[k] = move_group(kv[k], k)
     parts = []
+    ready = early(first, tokens, w_far)
     for part in range(2):
-        x = list(spread(part, first, tokens))
+        x = list(ready[4 * part : 4 * part + 4])
         for k in (1, 3, 2):
             x[k] = move_group(x[k], k)
         parts.append(x)
@@ -377,7 +459,10 @@
 
     mine, theirs = [], []
     for part in range(2):
-        q_mine, q_send = project(came, head0, parts[part], w_query)
+        if part:
+            q_mine, q_send = late(came, head0, parts[1])
+        else:
+            q_mine, q_send = project(came, head0, parts[0], w_query)
         mine.append(q_mine)
         theirs.append(move_seq(q_send, "swap"))
 

time: 108 us -> 110 us (1.019)
  local copies, waits for them, and re-layouts: 7.59 us -> 0.22 us
  starting transfers between devices: 41.5 us -> 47 us
  Pallas kernels: 24.7 us -> 27.6 us
    ppermute x19, starting transfers between devices: 30.3 us -> 38.1 us  [move_seq(): return lax.ppermute(a, 'seq', seq_moves(phase, k))]
    unnamed x28 -> x8, local copies, waits for them, and re-layouts: 7.4 us -> 0.02 us
    pallas_call x2, Pallas kernels: 1.46 us -> 8.49 us  [the longest x1 7.77 us: early(): pl.pallas_call(early_kernel, out_shape=(out,) * 8, in_specs=[pl.BlockSpec...]
    pallas_call x2 -> x1, Pallas kernels: 7.54 us -> 3.84 us  [project(): pl.pallas_call(project_kernel, out_shape=(out, out), in_specs=[smem, smem...]
    ppermute x9, starting transfers between devices: 11.2 us -> 8.93 us  [move_group(): lax.ppermute(a, 'group', [(g, (g + k) % GROUPS) for g in range(GROUPS)])]
    ppermute x9, waiting for transfers between devices: 22 us -> 23.5 us  [move_group(): lax.ppermute(a, 'group', [(g, (g + k) % GROUPS) for g in range(GROUPS)])]
    ppermute x19, waiting for transfers between devices: 11 us -> 9.69 us  [move_seq(): return lax.ppermute(a, 'seq', seq_moves(phase, k))]
  transfers between devices with their start and end apart: 28 -> 28, of which waited for: 11 -> 11; matrix products, arithmetic and copies ran while one was open for 0% -> 0% of each run, Pallas kernels for 18% -> 21%
where the time goes in v2:
time: 110 us; the launch traced here: 109 us
  starting transfers between devices  47 us (43%)
  waiting for transfers between devices  33.2 us (30%)
  Pallas kernels  27.6 us (25%)
    ppermute x19, starting transfers between devices, move_seq(): return lax.ppermute(a, 'seq', seq_moves(phase, k))  38.1 us
    ppermute x9, waiting for transfers between devices, move_group(): lax.ppermute(a, 'group', [(g, (g + k) % GROUPS) for g in range(GROUPS)])  23.5 us
    ppermute x19, waiting for transfers between devices, move_seq(): return lax.ppermute(a, 'seq', seq_moves(phase, k))  9.69 us
    pallas_call x2, Pallas kernels, attend(): pl.pallas_call(functools.partial(attend_kernel, rank), out_shape=(out, ou...  9.51 us
    ppermute x9, starting transfers between devices, move_group(): lax.ppermute(a, 'group', [(g, (g + k) % GROUPS) for g in range(GROUPS)])  8.93 us
    pallas_call x1, Pallas kernels, early(): pl.pallas_call(early_kernel, out_shape=(out,) * 8, in_specs=[pl.BlockSpec...  7.77 us
    pallas_call x1, Pallas kernels, project(): pl.pallas_call(project_kernel, out_shape=(out, out), in_specs=[smem, smem...  3.84 us
    pallas_call x1, Pallas kernels, pack(): pl.pallas_call(pack_kernel, out_shape=(kv,) * 4 + tuple(ints), in_specs=[...  2.89 us
  transfers between devices with their start and end apart: 28, of which 11 were waited for; matrix products, arithmetic and copies ran while one was open for 0% of the time, Pallas kernels for 21%

profile of v2, /device:TPU:1, one launch (start us, length us, event | category | flops | bytes accessed | tf_op | source)
XLA Modules:
  0.0 108.8 jit_solution(10149790012260744406)
XLA Ops:
  0.0 2.9 %shard_map.100 = (bf16[2,4,8,2048]{3,2,1,0:T(8,128)(2,1)S(1)}, bf16[2,4,8,2048]{3,2,1,0:T(8,128)(2,1)S(1)}, bf16[2,4,8,2048]{3,2,1,0:T(8,128)(2,1)S(1)}, bf16[2,...) custom-call(s32[6]{0:T(128)} %counts_ref.1, ...), custom_call_target="tpu_custom_call" | custom-call | flops 1000000 | bytes 2000000 | tf_op jit(solution)/shard_map/pallas_call | solution.py:119
  2.9 2.1 %collective-permute-start.8 = (bf16[2,4,8,2048]{3,2,1,0:T(8,128)(2,1)S(1)}, bf16[2,4,8,2048]{3,2,1,0:T(8,128)(2,1)S(1)}, u32[]{:S(2)}, u32[]{:S(2)}) collective-permute-start(bf16[2,4,8,2048]{3,2,1,0:T(8,128)(2,1)S(1)} %get-tuple-element.49), channel_id=1, source_target_pairs={{0,32},{32,64},{64,96},{96,0},{1,33},{33,65},{65,97},{97,1},{2,34}... | collective-permute-start | bytes 786440 | tf_op jit(solution)/shard_map/ppermute | solution.py:50
  5.0 2.4 %collective-permute-start.9 = (bf16[2,4,8,2048]{3,2,1,0:T(8,128)(2,1)S(1)}, bf16[2,4,8,2048]{3,2,1,0:T(8,128)(2,1)S(1)}, u32[]{:S(2)}, u32[]{:S(2)}) collective-permute-start(bf16[2,4,8,2048]{3,2,1,0:T(8,128)(2,1)S(1)} %get-tuple-element.50), channel_id=1, source_target_pairs={{0,64},{32,96},{64,0},{96,32},{1,65},{33,97},{65,1},{97,33},{2,66}... | collective-permute-start | bytes 786440 | tf_op jit(solution)/shard_map/ppermute | solution.py:50
  7.4 1.2 %collective-permute-start.10 = (bf16[2,4,8,2048]{3,2,1,0:T(8,128)(2,1)S(1)}, bf16[2,4,8,2048]{3,2,1,0:T(8,128)(2,1)S(1)}, u32[]{:S(2)}, u32[]{:S(2)}) collective-permute-start(bf16[2,4,8,2048]{3,2,1,0:T(8,128)(2,1)S(1)} %get-tuple-element.51), channel_id=1, source_target_pairs={{0,96},{32,0},{64,32},{96,64},{1,97},{33,1},{65,33},{97,65},{2,98}... | collective-permute-start | bytes 786440 | tf_op jit(solution)/shard_map/ppermute | solution.py:50
  8.5 7.8 %shard_map.101 = (bf16[4,32,2048]{2,1,0:T(8,128)(2,1)S(1)}, bf16[4,32,2048]{2,1,0:T(8,128)(2,1)S(1)}, bf16[4,32,2048]{2,1,0:T(8,128)(2,1)S(1)}, bf16[4,32,2048]{...) custom-call(s32[4]{0:T(128)S(1)} %get-tuple-element.35.first_ref, ...), custom_call_target="tpu_custom_call" | custom-call | flops 2150000128 | bytes 12000000 | tf_op jit(solution)/shard_map/pallas_call | solution.py:268
  16.7 0.9 collective-permute-start.1
  17.6 1.1 %collective-permute-done.9.kv2_ref = bf16[2,4,8,2048]{3,2,1,0:T(8,128)(2,1)S(1)} collective-permute-done((bf16[2,4,8,2048]{3,2,1,0:T(8,128)(2,1)S(1)}, bf16[2,4,8,2048]{3,2,1,0:T(8,128)(2,1)S(1)}, u32[]{:S(2)}, u32[]{:S(2)}) %collective-permute-start.9) | collective-permute-done | bytes 262176 | tf_op jit(solution)/shard_map/ppermute | solution.py:50
  18.7 1.0 shard_map.104
  19.7 2.7 %collective-permute-start.11 = (bf16[2,2,2,8,2048]{4,3,2,1,0:T(8,128)(2,1)S(1)}, bf16[2,2,2,8,2048]{4,3,2,1,0:T(8,128)(2,1)S(1)}, u32[]{:S(2)}, u32[]{:S(2)}) collective-permute-start(bf16[2,2,2,8,2048]{4,3,2,1,0:T(8,128)(2,1)S(1)} %get-tuple-element.53), channel_id=1, source_target_pairs={{0,1},{1,0},{2,3},{3,2},{4,5},{5,4},{6,7},{7,6},{8,9},{9,8},{10,11... | collective-permute-start | bytes 786440 | tf_op jit(solution)/shard_map/ppermute | solution.py:46
  22.4 1.1 %collective-permute-done.11 = bf16[2,2,2,8,2048]{4,3,2,1,0:T(8,128)(2,1)S(1)} collective-permute-done((bf16[2,2,2,8,2048]{4,3,2,1,0:T(8,128)(2,1)S(1)}, bf16[2,2,2,8,2048]{4,3,2,1,0:T(8,128)(2,1)S(1)}, u32[]{:S(2)}, u32[]{:S(2)}) %collective-permute-start.11) | collective-permute-done | bytes 262176 | tf_op jit(solution)/shard_map/ppermute | solution.py:46
  23.6 2.8 %collective-permute-start.14 = (bf16[2,2,16,2048]{3,2,1,0:T(8,128)(2,1)S(1)}, bf16[2,2,16,2048]{3,2,1,0:T(8,128)(2,1)S(1)}, u32[]{:S(2)}, u32[]{:S(2)}) collective-permute-start(bf16[2,2,16,2048]{3,2,1,0:T(8,128)(2,1)S(1)} %get-tuple-element.66), channel_id=1, source_target_pairs={{0,24},{1,7},{2,26},{3,1},{4,28},{5,3},{6,30},{7,5},{8,0},{9,15},{... | collective-permute-start | bytes 786440 | tf_op jit(solution)/shard_map/ppermute | solution.py:46
  27.5 2.8 %collective-permute-done.x1_ref = bf16[4,32,2048]{2,1,0:T(8,128)(2,1)S(1)} collective-permute-done((bf16[4,32,2048]{2,1,0:T(8,128)(2,1)S(1)}, bf16[4,32,2048]{2,1,0:T(8,128)(2,1)S(1)}, u32[]{:S(2)}, u32[]{:S(2)}) %collective-permute-start) | collective-permute-done | bytes 524320 | tf_op jit(solution)/shard_map/ppermute | solution.py:50
  30.4 2.2 %collective-permute-done.14 = bf16[2,2,16,2048]{3,2,1,0:T(8,128)(2,1)S(1)} collective-permute-done((bf16[2,2,16,2048]{3,2,1,0:T(8,128)(2,1)S(1)}, bf16[2,2,16,2048]{3,2,1,0:T(8,128)(2,1)S(1)}, u32[]{:S(2)}, u32[]{:S(2)}) %collective-permute-start.14) | collective-permute-done | bytes 262176 | tf_op jit(solution)/shard_map/ppermute | solution.py:46
  32.5 3.4 %collective-permute-start.21 = (bf16[2,2,16,2048]{3,2,1,0:T(8,128)(2,1)S(1)}, bf16[2,2,16,2048]{3,2,1,0:T(8,128)(2,1)S(1)}, u32[]{:S(2)}, u32[]{:S(2)}) collective-permute-start(bf16[2,2,16,2048]{3,2,1,0:T(8,128)(2,1)S(1)} %get-tuple-element.60), channel_id=1, source_target_pairs={{0,24},{1,7},{2,26},{3,1},{4,28},{5,3},{6,30},{7,5},{8,0},{9,15},{... | collective-permute-start | bytes 786440 | tf_op jit(solution)/shard_map/ppermute | solution.py:46
  36.7 4.7 %collective-permute-done.1.x2_ref = bf16[4,32,2048]{2,1,0:T(8,128)(2,1)S(1)} collective-permute-done((bf16[4,32,2048]{2,1,0:T(8,128)(2,1)S(1)}, bf16[4,32,2048]{2,1,0:T(8,128)(2,1)S(1)}, u32[]{:S(2)}, u32[]{:S(2)}) %collective-permute-start.1) | collective-permute-done | bytes 524320 | tf_op jit(solution)/shard_map/ppermute | solution.py:50
  42.1 2.0 %collective-permute-start.4 = (bf16[4,32,2048]{2,1,0:T(8,128)(2,1)S(1)}, bf16[4,32,2048]{2,1,0:T(8,128)(2,1)S(1)}, u32[]{:S(2)}, u32[]{:S(2)}) collective-permute-start(bf16[4,32,2048]{2,1,0:T(8,128)(2,1)S(1)} %get-tuple-element.43), channel_id=1, source_target_pairs={{0,64},{32,96},{64,0},{96,32},{1,65},{33,97},{65,1},{97,33},{2,66}... | collective-permute-start | bytes 1572872 | tf_op jit(solution)/shard_map/ppermute | solution.py:50
  44.0 1.5 %collective-permute-start.15 = (bf16[4,2,2,16,2048]{4,3,2,1,0:T(8,128)(2,1)S(1)}, bf16[4,2,2,16,2048]{4,3,2,1,0:T(8,128)(2,1)S(1)}, u32[]{:S(2)}, u32[]{:S(2)}) collective-permute-start(bf16[4,2,2,16,2048]{4,3,2,1,0:T(8,128)(2,1)S(1)} %pad_maximum_fusion.own_ref), channel_id=1, source_target_pairs={{0,2},{1,9},{2,4},{3,11},{4,6},{5,13},{6,0},{7,15},{8,10},{9,17},{... | collective-permute-start | bytes 3145736 | tf_op jit(solution)/shard_map/ppermute | solution.py:46
  45.5 3.7 %collective-permute-start.16 = (bf16[4,2,2,16,2048]{4,3,2,1,0:T(8,128)(2,1)S(1)}, bf16[4,2,2,16,2048]{4,3,2,1,0:T(8,128)(2,1)S(1)}, u32[]{:S(2)}, u32[]{:S(2)}) collective-permute-start(bf16[4,2,2,16,2048]{4,3,2,1,0:T(8,128)(2,1)S(1)} %pad_maximum_fusion.own_ref), channel_id=1, source_target_pairs={{0,6},{1,25},{2,0},{3,27},{4,2},{5,29},{6,4},{7,31},{8,14},{9,1},{... | collective-permute-start | bytes 3145736 | tf_op jit(solution)/shard_map/ppermute | solution.py:46
  49.5 8.5 %collective-permute-done.3.x1_ref = bf16[4,32,2048]{2,1,0:T(8,128)(2,1)S(1)} collective-permute-done((bf16[4,32,2048]{2,1,0:T(8,128)(2,1)S(1)}, bf16[4,32,2048]{2,1,0:T(8,128)(2,1)S(1)}, u32[]{:S(2)}, u32[]{:S(2)}) %collective-permute-start.3) | collective-permute-done | bytes 524320 | tf_op jit(solution)/shard_map/ppermute | solution.py:50
  58.0 3.2 %collective-permute-start.23 = (bf16[4,2,2,16,2048]{4,3,2,1,0:T(8,128)(2,1)S(1)}, bf16[4,2,2,16,2048]{4,3,2,1,0:T(8,128)(2,1)S(1)}, u32[]{:S(2)}, u32[]{:S(2)}) collective-permute-start(bf16[4,2,2,16,2048]{4,3,2,1,0:T(8,128)(2,1)S(1)} %pad_maximum_fusion.1.own_ref), channel_id=1, source_target_pairs={{0,6},{1,25},{2,0},{3,27},{4,2},{5,29},{6,4},{7,31},{8,14},{9,1},{... | collective-permute-start | bytes 3145736 | tf_op jit(solution)/shard_map/ppermute | solution.py:46
  61.1 3.8 %shard_map.102 = (bf16[4,32,2048]{2,1,0:T(8,128)(2,1)S(1)}, bf16[4,32,2048]{2,1,0:T(8,128)(2,1)S(1)}) custom-call(s32[2]{0:T(128)S(1)} %get-tuple-element.34.came_ref, s32[9]{0:T(128)S(1)} %get-tuple-element.33.head_ref, bf16[4,32,2048]{2,1,0:T(8,128)(2,1)S(1)} %get-tuple-element.36.x0_ref, bf16[4,32,2048]{2,1,0:T(8,128)(2,1)S(1)} %collective-permute-done.x1_ref, ...), custom_call_target="tpu_custom_call" | custom-call | flops 2150000128 | bytes 12000000 | tf_op jit(solution)/shard_map/pallas_call | solution.py:210
  65.0 6.4 %collective-permute-done.5.x3_ref = bf16[4,32,2048]{2,1,0:T(8,128)(2,1)S(1)} collective-permute-done((bf16[4,32,2048]{2,1,0:T(8,128)(2,1)S(1)}, bf16[4,32,2048]{2,1,0:T(8,128)(2,1)S(1)}, u32[]{:S(2)}, u32[]{:S(2)}) %collective-permute-start.5) | collective-permute-done | bytes 524320 | tf_op jit(solution)/shard_map/ppermute | solution.py:50
  71.4 9.4 %collective-permute-start.6 = (bf16[4,32,2048]{2,1,0:T(8,128)(2,1)S(1)}, bf16[4,32,2048]{2,1,0:T(8,128)(2,1)S(1)}, u32[]{:S(2)}, u32[]{:S(2)}) collective-permute-start(bf16[4,32,2048]{2,1,0:T(8,128)(2,1)S(1)} %get-tuple-element.46), channel_id=1, source_target_pairs={{0,1},{1,0},{2,3},{3,2},{4,5},{5,4},{6,7},{7,6},{8,9},{9,8},{10,11... | collective-permute-start | bytes 1572872 | tf_op jit(solution)/shard_map/ppermute | solution.py:46
  81.7 1.3 %collective-permute-start.17 = (bf16[2,2,2,16,2048]{4,3,2,1,0:T(8,128)(2,1)S(1)}, bf16[2,2,2,16,2048]{4,3,2,1,0:T(8,128)(2,1)S(1)}, u32[]{:S(2)}, u32[]{:S(2)}) collective-permute-start(bf16[2,2,2,16,2048]{4,3,2,1,0:T(8,128)(2,1)S(1)} %slice.33), channel_id=1, source_target_pairs={{0,2},{1,9},{2,4},{3,11},{4,6},{5,13},{6,0},{7,15},{8,10},{9,17},{... | collective-permute-start | bytes 1572872 | tf_op jit(solution)/shard_map/ppermute | solution.py:46
  83.0 2.8 %collective-permute-start.18 = (bf16[2,2,2,16,2048]{4,3,2,1,0:T(8,128)(2,1)S(1)}, bf16[2,2,2,16,2048]{4,3,2,1,0:T(8,128)(2,1)S(1)}, u32[]{:S(2)}, u32[]{:S(2)}) collective-permute-start(bf16[2,2,2,16,2048]{4,3,2,1,0:T(8,128)(2,1)S(1)} %slice.34), channel_id=1, source_target_pairs={{0,6},{1,25},{2,0},{3,27},{4,2},{5,29},{6,4},{7,31},{8,14},{9,1},{... | collective-permute-start | bytes 1572872 | tf_op jit(solution)/shard_map/ppermute | solution.py:46
  86.0 2.7 %collective-permute-start.25 = (bf16[2,2,2,16,2048]{4,3,2,1,0:T(8,128)(2,1)S(1)}, bf16[2,2,2,16,2048]{4,3,2,1,0:T(8,128)(2,1)S(1)}, u32[]{:S(2)}, u32[]{:S(2)}) collective-permute-start(bf16[2,2,2,16,2048]{4,3,2,1,0:T(8,128)(2,1)S(1)} %slice.37), channel_id=1, source_target_pairs={{0,6},{1,25},{2,0},{3,27},{4,2},{5,29},{6,4},{7,31},{8,14},{9,1},{... | collective-permute-start | bytes 1572872 | tf_op jit(solution)/shard_map/ppermute | solution.py:46
  88.7 3.8 %collective-permute-done.17.opa_ref = bf16[2,2,2,16,2048]{4,3,2,1,0:T(8,128)(2,1)S(1)} collective-permute-done((bf16[2,2,2,16,2048]{4,3,2,1,0:T(8,128)(2,1)S(1)}, bf16[2,2,2,16,2048]{4,3,2,1,0:T(8,128)(2,1)S(1)}, u32[]{:S(2)}, u32[]{:S(2)}) %collective-permute-start.17) | collective-permute-done | bytes 524320 | tf_op jit(solution)/shard_map/ppermute | solution.py:46
  92.5 4.7 %shard_map.105 = (bf16[2,64,2048]{2,1,0:T(8,128)(2,1)S(1)}, bf16[2,64,2048]{2,1,0:T(8,128)(2,1)S(1)}) custom-call(s32[9]{0:T(128)S(1)} %get-tuple-element.33.head_ref, bf16[4,32,2048]{2,1,0:T(8,128)(2,1)S(1)} %get-tuple-element.40.qm0_ref, bf16[4,32,2048]{2,1,0:T(8,128)(2,1)S(1)} %get-tuple-element.45.qm1_ref, ...), custom_call_target="tpu_custom_call" | custom-call | flops 3500000000 | bytes 14000000 | tf_op jit(solution)/shard_map/pallas_call | solution.py:372
  97.3 2.3 %collective-permute-start.26 = (bf16[2,64,2048]{2,1,0:T(8,128)(2,1)S(1)}, bf16[2,64,2048]{2,1,0:T(8,128)(2,1)S(1)}, u32[]{:S(2)}, u32[]{:S(2)}) collective-permute-start(bf16[2,64,2048]{2,1,0:T(8,128)(2,1)S(1)} %get-tuple-element.57), channel_id=1, source_target_pairs={{0,1},{1,0},{2,3},{3,2},{4,5},{5,4},{6,7},{7,6},{8,9},{9,8},{10,11... | collective-permute-start | bytes 1572872 | tf_op jit(solution)/shard_map/ppermute | solution.py:46
  99.6 4.8 %shard_map.106 = (bf16[2,64,2048]{2,1,0:T(8,128)(2,1)S(1)}, bf16[2,64,2048]{2,1,0:T(8,128)(2,1)S(1)}) custom-call(s32[9]{0:T(128)S(1)} %get-tuple-element.55.head_ref, bf16[4,32,2048]{2,1,0:T(8,128)(2,1)S(1)} %get-tuple-element.40.qm0_ref, bf16[4,32,2048]{2,1,0:T(8,128)(2,1)S(1)} %get-tuple-element.45.qm1_ref, ...), custom_call_target="tpu_custom_call" | custom-call | flops 3500000000 | bytes 14000000 | tf_op jit(solution)/shard_map/pallas_call | solution.py:372
  105.2 1.5 %collective-permute-done.27.t1_ref = bf16[2,64,2048]{2,1,0:T(8,128)(2,1)S(1)} collective-permute-done((bf16[2,64,2048]{2,1,0:T(8,128)(2,1)S(1)}, bf16[2,64,2048]{2,1,0:T(8,128)(2,1)S(1)}, u32[]{:S(2)}, u32[]{:S(2)}) %collective-permute-start.27) | collective-permute-done | bytes 524320 | tf_op jit(solution)/shard_map/ppermute | solution.py:46
  106.8 1.9 %shard_map.107 = bf16[8,64,2048]{2,1,0:T(8,128)(2,1)} custom-call(s32[8]{0:T(128)S(1)} %get-tuple-element.32.index_ref, bf16[2,64,2048]{2,1,0:T(8,128)(2,1)S(1)} %get-tuple-element.54.m0_ref, bf16[2,64,2048]{2,1,0:T(8,128)(2,1)S(1)} %get-tuple-element.56.m1_ref, bf16[2,64,2048]{2,1,0:T(8,128)(2,1)S(1)} %collective-permute-done.26.t0_ref, ...), custom_call_target="tpu_custom_call" | custom-call | flops 1000000 | bytes 4000000 | tf_op jit(solution)/shard_map/pallas_call | solution.py:405
  (52 shorter events, 5.2 us)
Async XLA Ops:
  2.9 14.7 %collective-permute-start.8 = (bf16[2,4,8,2048]{3,2,1,0:T(8,128)(2,1)S(1)}, bf16[2,4,8,2048]{3,2,1,0:T(8,128)(2,1)S(1)}, u32[]{:S(2)}, u32[]{:S(2)}) collective-permute-start(bf16[2,4,8,2048]{3,2,1,0:T(8,128)(2,1)S(1)} %get-tuple-element.49), channel_id=1, source_target_pairs={{0,32},{32,64},{64,96},{96,0},{1,33},{33,65},{65,97},{97,1},{2,34}... | collective-permute-start | bytes 786440 | tf_op jit(solution)/shard_map/ppermute | solution.py:50
  5.0 13.7 %collective-permute-start.9 = (bf16[2,4,8,2048]{3,2,1,0:T(8,128)(2,1)S(1)}, bf16[2,4,8,2048]{3,2,1,0:T(8,128)(2,1)S(1)}, u32[]{:S(2)}, u32[]{:S(2)}) collective-permute-start(bf16[2,4,8,2048]{3,2,1,0:T(8,128)(2,1)S(1)} %get-tuple-element.50), channel_id=1, source_target_pairs={{0,64},{32,96},{64,0},{96,32},{1,65},{33,97},{65,1},{97,33},{2,66}... | collective-permute-start | bytes 786440 | tf_op jit(solution)/shard_map/ppermute | solution.py:50
  7.4 11.3 %collective-permute-start.10 = (bf16[2,4,8,2048]{3,2,1,0:T(8,128)(2,1)S(1)}, bf16[2,4,8,2048]{3,2,1,0:T(8,128)(2,1)S(1)}, u32[]{:S(2)}, u32[]{:S(2)}) collective-permute-start(bf16[2,4,8,2048]{3,2,1,0:T(8,128)(2,1)S(1)} %get-tuple-element.51), channel_id=1, source_target_pairs={{0,96},{32,0},{64,32},{96,64},{1,97},{33,1},{65,33},{97,65},{2,98}... | collective-permute-start | bytes 786440 | tf_op jit(solution)/shard_map/ppermute | solution.py:50
  8.5 52.6 %slice-start = ((s8[8388608]{0:T(1024)(128)(4,1)}), s8[4194304]{0:T(1024)(128)(4,1)S(1)}, s32[]{:S(2)}) async-start(s8[8388608]{0:T(1024)(128)(4,1)} %bitcast.18), calls=%async_computation | async-start | bytes 8388608
  8.5 52.6 %slice-start.1 = ((s8[8388608]{0:T(1024)(128)(4,1)}), s8[4194304]{0:T(1024)(128)(4,1)S(1)}, s32[]{:S(2)}) async-start(s8[8388608]{0:T(1024)(128)(4,1)} %bitcast.18), calls=%async_computation.1 | async-start | bytes 8388608
  16.3 14.0 %collective-permute-start = (bf16[4,32,2048]{2,1,0:T(8,128)(2,1)S(1)}, bf16[4,32,2048]{2,1,0:T(8,128)(2,1)S(1)}, u32[]{:S(2)}, u32[]{:S(2)}) collective-permute-start(bf16[4,32,2048]{2,1,0:T(8,128)(2,1)S(1)} %get-tuple-element.37), channel_id=1, source_target_pairs={{0,32},{32,64},{64,96},{96,0},{1,33},{33,65},{65,97},{97,1},{2,34}... | collective-permute-start | bytes 1572872 | tf_op jit(solution)/shard_map/ppermute | solution.py:50
  16.7 24.6 %collective-permute-start.1 = (bf16[4,32,2048]{2,1,0:T(8,128)(2,1)S(1)}, bf16[4,32,2048]{2,1,0:T(8,128)(2,1)S(1)}, u32[]{:S(2)}, u32[]{:S(2)}) collective-permute-start(bf16[4,32,2048]{2,1,0:T(8,128)(2,1)S(1)} %get-tuple-element.38), channel_id=1, source_target_pairs={{0,64},{32,96},{64,0},{96,32},{1,65},{33,97},{65,1},{97,33},{2,66}... | collective-permute-start | bytes 1572872 | tf_op jit(solution)/shard_map/ppermute | solution.py:50
  19.7 3.8 %collective-permute-start.11 = (bf16[2,2,2,8,2048]{4,3,2,1,0:T(8,128)(2,1)S(1)}, bf16[2,2,2,8,2048]{4,3,2,1,0:T(8,128)(2,1)S(1)}, u32[]{:S(2)}, u32[]{:S(2)}) collective-permute-start(bf16[2,2,2,8,2048]{4,3,2,1,0:T(8,128)(2,1)S(1)} %get-tuple-element.53), channel_id=1, source_target_pairs={{0,1},{1,0},{2,3},{3,2},{4,5},{5,4},{6,7},{7,6},{8,9},{9,8},{10,11... | collective-permute-start | bytes 786440 | tf_op jit(solution)/shard_map/ppermute | solution.py:46
  23.6 8.9 %collective-permute-start.14 = (bf16[2,2,16,2048]{3,2,1,0:T(8,128)(2,1)S(1)}, bf16[2,2,16,2048]{3,2,1,0:T(8,128)(2,1)S(1)}, u32[]{:S(2)}, u32[]{:S(2)}) collective-permute-start(bf16[2,2,16,2048]{3,2,1,0:T(8,128)(2,1)S(1)} %get-tuple-element.66), channel_id=1, source_target_pairs={{0,24},{1,7},{2,26},{3,1},{4,28},{5,3},{6,30},{7,5},{8,0},{9,15},{... | collective-permute-start | bytes 786440 | tf_op jit(solution)/shard_map/ppermute | solution.py:46
  26.4 9.5 %collective-permute-start.13 = (bf16[2,2,16,2048]{3,2,1,0:T(8,128)(2,1)S(1)}, bf16[2,2,16,2048]{3,2,1,0:T(8,128)(2,1)S(1)}, u32[]{:S(2)}, u32[]{:S(2)}) collective-permute-start(bf16[2,2,16,2048]{3,2,1,0:T(8,128)(2,1)S(1)} %get-tuple-element.66), channel_id=1, source_target_pairs={{0,16},{1,5},{2,18},{3,7},{4,20},{5,1},{6,22},{7,3},{8,24},{9,13},... | collective-permute-start | bytes 786440 | tf_op jit(solution)/shard_map/ppermute | solution.py:46
  26.8 9.5 %collective-permute-start.12 = (bf16[2,2,16,2048]{3,2,1,0:T(8,128)(2,1)S(1)}, bf16[2,2,16,2048]{3,2,1,0:T(8,128)(2,1)S(1)}, u32[]{:S(2)}, u32[]{:S(2)}) collective-permute-start(bf16[2,2,16,2048]{3,2,1,0:T(8,128)(2,1)S(1)} %get-tuple-element.66), channel_id=1, source_target_pairs={{0,8},{1,3},{2,10},{3,5},{4,12},{5,7},{6,14},{7,1},{8,16},{9,11},{... | collective-permute-start | bytes 786440 | tf_op jit(solution)/shard_map/ppermute | solution.py:46
  30.3 19.1 %collective-permute-start.2 = (bf16[4,32,2048]{2,1,0:T(8,128)(2,1)S(1)}, bf16[4,32,2048]{2,1,0:T(8,128)(2,1)S(1)}, u32[]{:S(2)}, u32[]{:S(2)}) collective-permute-start(bf16[4,32,2048]{2,1,0:T(8,128)(2,1)S(1)} %get-tuple-element.39), channel_id=1, source_target_pairs={{0,96},{32,0},{64,32},{96,64},{1,97},{33,1},{65,33},{97,65},{2,98}... | collective-permute-start | bytes 1572872 | tf_op jit(solution)/shard_map/ppermute | solution.py:50
  32.5 9.5 %collective-permute-start.21 = (bf16[2,2,16,2048]{3,2,1,0:T(8,128)(2,1)S(1)}, bf16[2,2,16,2048]{3,2,1,0:T(8,128)(2,1)S(1)}, u32[]{:S(2)}, u32[]{:S(2)}) collective-permute-start(bf16[2,2,16,2048]{3,2,1,0:T(8,128)(2,1)S(1)} %get-tuple-element.60), channel_id=1, source_target_pairs={{0,24},{1,7},{2,26},{3,1},{4,28},{5,3},{6,30},{7,5},{8,0},{9,15},{... | collective-permute-start | bytes 786440 | tf_op jit(solution)/shard_map/ppermute | solution.py:46
  36.0 8.1 %collective-permute-start.20 = (bf16[2,2,16,2048]{3,2,1,0:T(8,128)(2,1)S(1)}, bf16[2,2,16,2048]{3,2,1,0:T(8,128)(2,1)S(1)}, u32[]{:S(2)}, u32[]{:S(2)}) collective-permute-start(bf16[2,2,16,2048]{3,2,1,0:T(8,128)(2,1)S(1)} %get-tuple-element.60), channel_id=1, source_target_pairs={{0,16},{1,5},{2,18},{3,7},{4,20},{5,1},{6,22},{7,3},{8,24},{9,13},... | collective-permute-start | bytes 786440 | tf_op jit(solution)/shard_map/ppermute | solution.py:46
  36.2 9.3 %collective-permute-start.19 = (bf16[2,2,16,2048]{3,2,1,0:T(8,128)(2,1)S(1)}, bf16[2,2,16,2048]{3,2,1,0:T(8,128)(2,1)S(1)}, u32[]{:S(2)}, u32[]{:S(2)}) collective-permute-start(bf16[2,2,16,2048]{3,2,1,0:T(8,128)(2,1)S(1)} %get-tuple-element.60), channel_id=1, source_target_pairs={{0,8},{1,3},{2,10},{3,5},{4,12},{5,7},{6,14},{7,1},{8,16},{9,11},{... | collective-permute-start | bytes 786440 | tf_op jit(solution)/shard_map/ppermute | solution.py:46
  41.3 16.6 %collective-permute-start.3 = (bf16[4,32,2048]{2,1,0:T(8,128)(2,1)S(1)}, bf16[4,32,2048]{2,1,0:T(8,128)(2,1)S(1)}, u32[]{:S(2)}, u32[]{:S(2)}) collective-permute-start(bf16[4,32,2048]{2,1,0:T(8,128)(2,1)S(1)} %get-tuple-element.42), channel_id=1, source_target_pairs={{0,32},{32,64},{64,96},{96,0},{1,33},{33,65},{65,97},{97,1},{2,34}... | collective-permute-start | bytes 1572872 | tf_op jit(solution)/shard_map/ppermute | solution.py:50
  42.1 19.0 %collective-permute-start.4 = (bf16[4,32,2048]{2,1,0:T(8,128)(2,1)S(1)}, bf16[4,32,2048]{2,1,0:T(8,128)(2,1)S(1)}, u32[]{:S(2)}, u32[]{:S(2)}) collective-permute-start(bf16[4,32,2048]{2,1,0:T(8,128)(2,1)S(1)} %get-tuple-element.43), channel_id=1, source_target_pairs={{0,64},{32,96},{64,0},{96,32},{1,65},{33,97},{65,1},{97,33},{2,66}... | collective-permute-start | bytes 1572872 | tf_op jit(solution)/shard_map/ppermute | solution.py:50
  44.0 37.5 %collective-permute-start.15 = (bf16[4,2,2,16,2048]{4,3,2,1,0:T(8,128)(2,1)S(1)}, bf16[4,2,2,16,2048]{4,3,2,1,0:T(8,128)(2,1)S(1)}, u32[]{:S(2)}, u32[]{:S(2)}) collective-permute-start(bf16[4,2,2,16,2048]{4,3,2,1,0:T(8,128)(2,1)S(1)} %pad_maximum_fusion.own_ref), channel_id=1, source_target_pairs={{0,2},{1,9},{2,4},{3,11},{4,6},{5,13},{6,0},{7,15},{8,10},{9,17},{... | collective-permute-start | bytes 3145736 | tf_op jit(solution)/shard_map/ppermute | solution.py:46
  45.5 36.1 %collective-permute-start.16 = (bf16[4,2,2,16,2048]{4,3,2,1,0:T(8,128)(2,1)S(1)}, bf16[4,2,2,16,2048]{4,3,2,1,0:T(8,128)(2,1)S(1)}, u32[]{:S(2)}, u32[]{:S(2)}) collective-permute-start(bf16[4,2,2,16,2048]{4,3,2,1,0:T(8,128)(2,1)S(1)} %pad_maximum_fusion.own_ref), channel_id=1, source_target_pairs={{0,6},{1,25},{2,0},{3,27},{4,2},{5,29},{6,4},{7,31},{8,14},{9,1},{... | collective-permute-start | bytes 3145736 | tf_op jit(solution)/shard_map/ppermute | solution.py:46
  49.2 43.2 %slice-start.2 = ((s8[8388608]{0:T(1024)(128)(4,1)}), s8[4194304]{0:T(1024)(128)(4,1)S(1)}, s32[]{:S(2)}) async-start(s8[8388608]{0:T(1024)(128)(4,1)} %bitcast.20), calls=%async_computation.2 | async-start | bytes 8388608
  49.4 33.6 %collective-permute-start.22 = (bf16[4,2,2,16,2048]{4,3,2,1,0:T(8,128)(2,1)S(1)}, bf16[4,2,2,16,2048]{4,3,2,1,0:T(8,128)(2,1)S(1)}, u32[]{:S(2)}, u32[]{:S(2)}) collective-permute-start(bf16[4,2,2,16,2048]{4,3,2,1,0:T(8,128)(2,1)S(1)} %pad_maximum_fusion.1.own_ref), channel_id=1, source_target_pairs={{0,2},{1,9},{2,4},{3,11},{4,6},{5,13},{6,0},{7,15},{8,10},{9,17},{... | collective-permute-start | bytes 3145736 | tf_op jit(solution)/shard_map/ppermute | solution.py:46
  58.0 27.9 %collective-permute-start.23 = (bf16[4,2,2,16,2048]{4,3,2,1,0:T(8,128)(2,1)S(1)}, bf16[4,2,2,16,2048]{4,3,2,1,0:T(8,128)(2,1)S(1)}, u32[]{:S(2)}, u32[]{:S(2)}) collective-permute-start(bf16[4,2,2,16,2048]{4,3,2,1,0:T(8,128)(2,1)S(1)} %pad_maximum_fusion.1.own_ref), channel_id=1, source_target_pairs={{0,6},{1,25},{2,0},{3,27},{4,2},{5,29},{6,4},{7,31},{8,14},{9,1},{... | collective-permute-start | bytes 3145736 | tf_op jit(solution)/shard_map/ppermute | solution.py:46
  61.1 10.3 %collective-permute-start.5 = (bf16[4,32,2048]{2,1,0:T(8,128)(2,1)S(1)}, bf16[4,32,2048]{2,1,0:T(8,128)(2,1)S(1)}, u32[]{:S(2)}, u32[]{:S(2)}) collective-permute-start(bf16[4,32,2048]{2,1,0:T(8,128)(2,1)S(1)} %get-tuple-element.44), channel_id=1, source_target_pairs={{0,96},{32,0},{64,32},{96,64},{1,97},{33,1},{65,33},{97,65},{2,98}... | collective-permute-start | bytes 1572872 | tf_op jit(solution)/shard_map/ppermute | solution.py:50
  61.1 31.4 %slice-start.3 = ((s8[8388608]{0:T(1024)(128)(4,1)}), s8[4194304]{0:T(1024)(128)(4,1)S(1)}, s32[]{:S(2)}) async-start(s8[8388608]{0:T(1024)(128)(4,1)} %bitcast.20), calls=%async_computation.3 | async-start | bytes 8388608
  71.4 14.6 %collective-permute-start.6 = (bf16[4,32,2048]{2,1,0:T(8,128)(2,1)S(1)}, bf16[4,32,2048]{2,1,0:T(8,128)(2,1)S(1)}, u32[]{:S(2)}, u32[]{:S(2)}) collective-permute-start(bf16[4,32,2048]{2,1,0:T(8,128)(2,1)S(1)} %get-tuple-element.46), channel_id=1, source_target_pairs={{0,1},{1,0},{2,3},{3,2},{4,5},{5,4},{6,7},{7,6},{8,9},{9,8},{10,11... | collective-permute-start | bytes 1572872 | tf_op jit(solution)/shard_map/ppermute | solution.py:46
  81.5 7.2 %collective-permute-start.7 = (bf16[4,32,2048]{2,1,0:T(8,128)(2,1)S(1)}, bf16[4,32,2048]{2,1,0:T(8,128)(2,1)S(1)}, u32[]{:S(2)}, u32[]{:S(2)}) collective-permute-start(bf16[4,32,2048]{2,1,0:T(8,128)(2,1)S(1)} %get-tuple-element.47), channel_id=1, source_target_pairs={{0,1},{1,0},{2,3},{3,2},{4,5},{5,4},{6,7},{7,6},{8,9},{9,8},{10,11... | collective-permute-start | bytes 1572872 | tf_op jit(solution)/shard_map/ppermute | solution.py:46
  81.7 10.8 %collective-permute-start.17 = (bf16[2,2,2,16,2048]{4,3,2,1,0:T(8,128)(2,1)S(1)}, bf16[2,2,2,16,2048]{4,3,2,1,0:T(8,128)(2,1)S(1)}, u32[]{:S(2)}, u32[]{:S(2)}) collective-permute-start(bf16[2,2,2,16,2048]{4,3,2,1,0:T(8,128)(2,1)S(1)} %slice.33), channel_id=1, source_target_pairs={{0,2},{1,9},{2,4},{3,11},{4,6},{5,13},{6,0},{7,15},{8,10},{9,17},{... | collective-permute-start | bytes 1572872 | tf_op jit(solution)/shard_map/ppermute | solution.py:46
  83.0 9.5 %collective-permute-start.18 = (bf16[2,2,2,16,2048]{4,3,2,1,0:T(8,128)(2,1)S(1)}, bf16[2,2,2,16,2048]{4,3,2,1,0:T(8,128)(2,1)S(1)}, u32[]{:S(2)}, u32[]{:S(2)}) collective-permute-start(bf16[2,2,2,16,2048]{4,3,2,1,0:T(8,128)(2,1)S(1)} %slice.34), channel_id=1, source_target_pairs={{0,6},{1,25},{2,0},{3,27},{4,2},{5,29},{6,4},{7,31},{8,14},{9,1},{... | collective-permute-start | bytes 1572872 | tf_op jit(solution)/shard_map/ppermute | solution.py:46
  85.8 13.8 %collective-permute-start.24 = (bf16[2,2,2,16,2048]{4,3,2,1,0:T(8,128)(2,1)S(1)}, bf16[2,2,2,16,2048]{4,3,2,1,0:T(8,128)(2,1)S(1)}, u32[]{:S(2)}, u32[]{:S(2)}) collective-permute-start(bf16[2,2,2,16,2048]{4,3,2,1,0:T(8,128)(2,1)S(1)} %slice.36), channel_id=1, source_target_pairs={{0,2},{1,9},{2,4},{3,11},{4,6},{5,13},{6,0},{7,15},{8,10},{9,17},{... | collective-permute-start | bytes 1572872 | tf_op jit(solution)/shard_map/ppermute | solution.py:46
  86.0 13.6 %collective-permute-start.25 = (bf16[2,2,2,16,2048]{4,3,2,1,0:T(8,128)(2,1)S(1)}, bf16[2,2,2,16,2048]{4,3,2,1,0:T(8,128)(2,1)S(1)}, u32[]{:S(2)}, u32[]{:S(2)}) collective-permute-start(bf16[2,2,2,16,2048]{4,3,2,1,0:T(8,128)(2,1)S(1)} %slice.37), channel_id=1, source_target_pairs={{0,6},{1,25},{2,0},{3,27},{4,2},{5,29},{6,4},{7,31},{8,14},{9,1},{... | collective-permute-start | bytes 1572872 | tf_op jit(solution)/shard_map/ppermute | solution.py:46
  97.3 8.0 %collective-permute-start.26 = (bf16[2,64,2048]{2,1,0:T(8,128)(2,1)S(1)}, bf16[2,64,2048]{2,1,0:T(8,128)(2,1)S(1)}, u32[]{:S(2)}, u32[]{:S(2)}) collective-permute-start(bf16[2,64,2048]{2,1,0:T(8,128)(2,1)S(1)} %get-tuple-element.57), channel_id=1, source_target_pairs={{0,1},{1,0},{2,3},{3,2},{4,5},{5,4},{6,7},{7,6},{8,9},{9,8},{10,11... | collective-permute-start | bytes 1572872 | tf_op jit(solution)/shard_map/ppermute | solution.py:46
  104.4 2.4 %collective-permute-start.27 = (bf16[2,64,2048]{2,1,0:T(8,128)(2,1)S(1)}, bf16[2,64,2048]{2,1,0:T(8,128)(2,1)S(1)}, u32[]{:S(2)}, u32[]{:S(2)}) collective-permute-start(bf16[2,64,2048]{2,1,0:T(8,128)(2,1)S(1)} %get-tuple-element.58), channel_id=1, source_target_pairs={{0,1},{1,0},{2,3},{3,2},{4,5},{5,4},{6,7},{7,6},{8,9},{9,8},{10,11... | collective-permute-start | bytes 1572872 | tf_op jit(solution)/shard_map/ppermute | solution.py:46
